TPU v7x, 32 devices: a whole 2x2x4 slice. The times are simulated.
32 devices in a mesh: level: 2 (over x), subj: 4 (over y, core), gz: 4 (over z).
Axes of the slice: x: 2, y: 2, z: 4, core: 2. Of those that a mesh axis runs over, the one named last changes fastest.
Arguments:
- images: bfloat16 [8, 192, 192, 192], P('subj', 'gz'), may hold values from -6 to 6
- momenta: float32 [8, 96, 3, 96, 96], P('subj', 'gz'), may hold values from -18 to 18
- assign: int32 [8], replicated, may hold values from 0 to 7, as said below
Outputs:
- template: float32 [192, 192, 192], P('gz')
Inputs may be any that keep to these rules, and one draw needn't show every extreme that they name: assign is a permutation of 0 to 7 with assign[i] % 2 == i % 2 for every i.
All inputs are finite; a program needn't handle non-finite values.
Results may differ from a plain program's by a relative error of at most 0.00069.
Values may be sent and summed in bfloat16 or wider, within the bound.
A program may use at most 128 MiB of HBM per device.

v0:
```python
import jax
import jax.numpy as jnp
from jax import lax
from jax.experimental import pallas as pl
from jax.experimental.pallas import tpu as pltpu
from jax.sharding import PartitionSpec as P

SWEEPS = 2


def with_halo(array, sides, width):
    for axis, dim in sides:
        size, length = (lax.axis_size(axis), array.shape[dim])
        up = [(i, (i + 1) % size) for i in range(size - 1)]
        down = [(j, i) for i, j in up]
        last = lax.slice_in_dim(array, length - width, length, axis=dim)
        leading = lax.slice_in_dim(array, 0, width, axis=dim)
        before = lax.ppermute(last, axis, up)
        after = lax.ppermute(leading, axis, down)
        array = jnp.concatenate([before, array, after], axis=dim)
    return array


def band(padded, count, axis):

    def take(offset):
        return lax.slice_in_dim(padded, offset, offset + count, axis=axis)

    return (take(0) + take(4)) * 0.0625 + (take(1) + take(3)) * 0.25 + take(2) * 0.375


def blur_plane(field, axis):
    widths = [(2, 2) if dimension == axis else (0, 0) for dimension in range(field.ndim)]
    return band(jnp.pad(field, widths), field.shape[axis], axis)


def upsample_table(finest, coarse, offset):
    rows_fine = jnp.arange(finest, dtype=jnp.int32)[:, None]
    columns = jnp.arange(coarse, dtype=jnp.int32)[None, :]
    nearest = rows_fine // 2 + offset
    farther = nearest + 2 * (rows_fine % 2) - 1
    return 0.75 * (columns == nearest).astype(jnp.float32) + 0.25 * (columns == farther).astype(
        jnp.float32
    )


def halo_rows(first, last, axis):
    size = lax.axis_size(axis)
    up = [(i, (i + 1) % size) for i in range(size - 1)]
    down = [(j, i) for i, j in up]
    return lax.ppermute(last, axis, up), lax.ppermute(first, axis, down)


def slope_table(finest):
    rows = jnp.arange(finest, dtype=jnp.int32)[:, None]
    columns = jnp.arange(finest, dtype=jnp.int32)[None, :]
    ahead = (columns == rows + 1).astype(jnp.float32)
    behind = (columns == rows - 1).astype(jnp.float32)
    return ((ahead - behind) * 0.5).astype(jnp.bfloat16)


LANES = 128


def pack_coarse(field):
    coarse = field.shape[-1]
    rest = LANES - coarse
    kept = coarse * coarse // LANES
    tail = field[..., kept:, :]
    pieces = [tail[..., i : i + rest] for i in range(0, coarse, rest)]
    return jnp.concatenate([field[..., :kept, :], jnp.concatenate(pieces, axis=-2)], axis=-1)


def warp_kernel(
    sel, velocity, pair, below, above, before, after, up_x, up_y, slope_x, slope_y, out, fine
):
    step = pl.program_id(0)
    last = pl.num_programs(0) - 1
    for c in range(3):
        packed = velocity[0, 0, c]
        parts = [
            jnp.dot(packed, up_x[i], preferred_element_type=jnp.float32)
            for i in range(up_x.shape[0])
        ]
        size = packed.shape[0] // (len(parts) - 1)
        tail = parts[1][:size]
        for i in range(2, len(parts)):
            tail = tail + parts[i][(i - 1) * size : i * size]
        wide = jnp.concatenate([parts[0], tail], axis=0)
        high = wide.astype(jnp.bfloat16)
        low = (wide - high.astype(jnp.float32)).astype(jnp.bfloat16)
        both = jnp.concatenate([high, low], axis=0)
        fine[lax.rem(step, 3), c] = jnp.dot(up_y[...], both, preferred_element_type=jnp.float32)

    @pl.when(step >= 2)
    def _():
        finest = pair.shape[2]
        half = finest // 2
        rest = finest - LANES
        chunk = finest // 4
        scale = sel[2].astype(jnp.float32) * (1.0 / sel[3].astype(jnp.float32))
        middle = lax.rem(step + 2, 3)
        prior_is_halo = step == 2
        next_is_halo = step == last
        for z in range(2):
            outer = lax.rem(step + 1, 3) if z == 0 else lax.rem(step, 3)
            for r in range(0, finest, chunk):
                rows = pl.ds(r, chunk)
                image = pair[0, z, rows, :]
                dx = jnp.dot(image, slope_x[...], preferred_element_type=jnp.float32)
                dy = jnp.dot(
                    slope_y[rows, :], pair[0, z], preferred_element_type=jnp.float32
                )
                if z == 0:
                    back = jnp.where(
                        prior_is_halo,
                        before[0, rows, :].astype(jnp.float32),
                        below[0, 0, rows, :].astype(jnp.float32),
                    )
                    ahead = pair[0, 1, rows, :].astype(jnp.float32)
                else:
                    back = pair[0, 0, rows, :].astype(jnp.float32)
                    ahead = jnp.where(
                        next_is_halo,
                        after[0, rows, :].astype(jnp.float32),
                        above[0, 0, rows, :].astype(jnp.float32),
                    )
                dz = (ahead - back) * 0.5
                near = (
                    fine[middle, 0, rows, :] * dx
                    + fine[middle, 1, rows, :] * dy
                    + fine[middle, 2, rows, :] * dz
                )
                far = (
                    fine[outer, 0, rows, :] * dx
                    + fine[outer, 1, rows, :] * dy
                    + fine[outer, 2, rows, :] * dz
                )
                value = scale * (image.astype(jnp.float32) - (0.75 * near + 0.25 * far))
                out[z, rows, :] = value[:, :LANES]
                side = rest * (r // half)
                out[z, pl.ds(finest + r % half, chunk), side : side + rest] = value[:, LANES:]


def warp(sel, gathered, images, before, after, interpret=False):
    finest = images.shape[2]
    slab_ext, kept = gathered.shape[1], gathered.shape[3]
    coarse = finest // 2
    rest = LANES - coarse
    fine_slab = images.shape[1]
    table = upsample_table(finest, coarse, 0).astype(jnp.bfloat16)
    columns = table.T
    up_x = [jnp.pad(columns, ((0, rest), (0, 0)))]
    for i in range(0, coarse, rest):
        up_x.append(jnp.pad(columns[i : i + rest], ((coarse, 0), (0, 0))))
    up_x = jnp.stack(up_x)
    slope = slope_table(finest)
    whole = lambda j, s: (0, 0)
    edge = lambda j, s: (0, 0, 0)
    lag = lambda j: jnp.maximum(j - 2, 0)
    plane = (1, 1, finest, finest)
    grid_spec = pltpu.PrefetchScalarGridSpec(
        num_scalar_prefetch=1,
        grid=(slab_ext,),
        in_specs=[
            pl.BlockSpec((1, 1, 3, kept, LANES), lambda j, s: (s[1], j, 0, 0, 0)),
            pl.BlockSpec((1, 2, finest, finest), lambda j, s: (s[0], lag(j), 0, 0)),
            pl.BlockSpec(plane, lambda j, s: (s[0], jnp.maximum(2 * lag(j) - 1, 0), 0, 0)),
            pl.BlockSpec(
                plane, lambda j, s: (s[0], jnp.minimum(2 * lag(j) + 2, fine_slab - 1), 0, 0)
            ),
            pl.BlockSpec((1, finest, finest), edge),
            pl.BlockSpec((1, finest, finest), edge),
            pl.BlockSpec(up_x.shape, edge),
            pl.BlockSpec((finest, 2 * coarse), whole),
            pl.BlockSpec((finest, finest), whole),
            pl.BlockSpec((finest, finest), whole),
        ],
        out_specs=pl.BlockSpec(
            (2, finest + finest // 2, LANES), lambda j, s: (lag(j), 0, 0)
        ),
        scratch_shapes=[pltpu.VMEM((3, 3, finest, finest), jnp.float32)],
    )
    return pl.pallas_call(
        warp_kernel,
        grid_spec=grid_spec,
        out_shape=jax.ShapeDtypeStruct((fine_slab, finest + finest // 2, LANES), jnp.float32),
        compiler_params=pltpu.CompilerParams(dimension_semantics=("arbitrary",)),
        interpret=interpret,
    )(
        sel,
        gathered,
        images,
        images,
        images,
        before,
        after,
        up_x,
        jnp.concatenate([table, table], axis=1),
        slope.T,
        slope,
    )


MARGIN = 8


def relax_row(ref, slot, behind, ahead, r, chunk):
    rows = pl.ds(MARGIN + r, chunk)
    center = ref[slot, rows, :]
    width = center.shape[1]
    neighbours = (
        ref[behind, rows, :]
        + ref[ahead, rows, :]
        + ref[slot, pl.ds(MARGIN + r - 1, chunk), :]
        + ref[slot, pl.ds(MARGIN + r + 1, chunk), :]
        + pltpu.roll(center, 1, 1)
        + pltpu.roll(center, width - 1, 1)
    )
    return center + 0.15 * (neighbours - 6.0 * center)


def sweep_kernel(sel, mean, before, after, out, first, second):
    step = pl.program_id(0)
    last = pl.num_programs(0) - 1
    finest = out.shape[1]
    half = finest // 2
    rest = finest - LANES
    chunk = finest // 3
    base = 2 * lax.rem(step, 2)
    other = 2 - base

    def enter(ref):
        for z in range(2):
            slot = base + z
            first[slot, pl.ds(MARGIN, finest), 0:LANES] = ref[z, 0:finest, :]
            side = ref[z, finest : finest + half, :]
            first[slot, pl.ds(MARGIN, half), LANES:finest] = side[:, :rest]
            turned = pltpu.roll(side, LANES - rest, 1)
            first[slot, pl.ds(MARGIN + half, half), LANES:finest] = turned[:, :rest]

    @pl.when(step == 0)
    def _():
        first[...] = jnp.zeros_like(first)
        second[...] = jnp.zeros_like(second)
        enter(before)

    @pl.when((step > 0) & (step < last))
    def _():
        enter(mean)

    @pl.when(step == last)
    def _():
        enter(after)

    @pl.when(step >= 1)
    def _():
        keep_low = jnp.where((step == 1) & (sel[0] == 0), 0.0, 1.0)
        keep_high = jnp.where((step == last) & (sel[0] == sel[1]), 0.0, 1.0)
        places = ((other + 1, other, base, keep_low), (base, other + 1, base + 1, keep_high))
        for slot, behind, ahead, keep in places:
            for r in range(0, finest, chunk):
                value = relax_row(first, slot, behind, ahead, r, chunk) * keep
                second[slot, pl.ds(MARGIN + r, chunk), 0:finest] = value[:, :finest]

    @pl.when(step >= 2)
    def _():
        places = ((other, base + 1, other + 1), (other + 1, other, base))
        for z, (slot, behind, ahead) in enumerate(places):
            for r in range(0, finest, chunk):
                value = relax_row(second, slot, behind, ahead, r, chunk)
                out[z, pl.ds(r, chunk), :] = value[:, :finest]


def sweeps(sel, mean, before, after, finest, interpret=False):
    fine_slab = mean.shape[0]
    blocks = fine_slab // 2
    block = (2,) + mean.shape[1:]
    width = -(-(finest + 1) // LANES) * LANES
    ring = pltpu.VMEM((4, finest + 2 * MARGIN, width), jnp.float32)
    grid_spec = pltpu.PrefetchScalarGridSpec(
        num_scalar_prefetch=1,
        grid=(blocks + 2,),
        in_specs=[
            pl.BlockSpec(block, lambda j, s: (jnp.clip(j - 1, 0, blocks - 1), 0, 0)),
            pl.BlockSpec(block, lambda j, s: (0, 0, 0)),
            pl.BlockSpec(block, lambda j, s: (0, 0, 0)),
        ],
        out_specs=pl.BlockSpec(
            (2, finest, finest), lambda j, s: (jnp.maximum(j - 2, 0), 0, 0)
        ),
        scratch_shapes=[ring, ring],
    )
    return pl.pallas_call(
        sweep_kernel,
        grid_spec=grid_spec,
        out_shape=jax.ShapeDtypeStruct((fine_slab, finest, finest), jnp.float32),
        compiler_params=pltpu.CompilerParams(dimension_semantics=("arbitrary",)),
        interpret=interpret,
    )(sel, mean, before, after)


def shards(images, momenta, assign):
    count = momenta.shape[0]
    slab = momenta.shape[1]
    coarse = momenta.shape[3]
    finest = images.shape[2]
    fine_slab = images.shape[1]
    level_index = lax.axis_index("level")
    group_index = lax.axis_index("subj")
    zone_index = lax.axis_index("gz")
    rim_width = 3
    ticker = 0 + level_index
    weight = (ticker < count).astype(jnp.int32)
    ticker = jnp.minimum(ticker, count - 1)
    moment = lax.dynamic_index_in_dim(momenta, ticker, 0, keepdims=False)
    extended = with_halo(moment, (("gz", 0),), rim_width)
    smooth = blur_plane(blur_plane(extended, 3), 2)
    field = band(smooth, extended.shape[0] - 4, 0)
    global_z = zone_index * slab - 1 + jnp.arange(field.shape[0], dtype=jnp.int32)
    inside = (global_z >= 0) & (global_z < slab * lax.axis_size("gz"))
    field = jnp.where(inside[:, None, None, None], field, 0.0)
    field = pack_coarse(field.astype(jnp.bfloat16))
    source = assign[group_index * count + ticker] // count
    piece = lax.all_gather(field[None], "subj", axis=0, tiled=True)
    rows = lax.dynamic_slice_in_dim(images, ticker, 1, 0)
    image_before, image_after = halo_rows(rows[0, :1], rows[0, fine_slab - 1 :], "gz")
    subjects = jnp.int32(lax.axis_size("subj") * count)
    sel = jnp.stack([ticker, source, weight, subjects]).astype(jnp.int32)
    total = warp(sel, piece, images, image_before, image_after)
    mean = lax.psum(total, ("level", "subj"))
    mean_before, mean_after = halo_rows(mean[:2], mean[fine_slab - 2 :], "gz")
    zones = jnp.stack([zone_index, lax.axis_size("gz") - 1]).astype(jnp.int32)
    return sweeps(zones, mean, mean_before, mean_after, finest)


def solution(mesh):
    return jax.shard_map(
        shards,
        mesh=mesh,
        in_specs=(P("subj", "gz", None, None), P("subj", "gz", None, None, None), P()),
        out_specs=P("gz", None, None),
        check_vma=False,
    )
```

profile of v0, /device:TPU:0, one launch (start us, length us, event | category | flops | bytes accessed | tf_op | source)
XLA Modules:
  0.0 278.5 jit_solution(7556803504424575824)
XLA Ops:
  6.5 1.2 dynamic-slice_bitcast_fusion.2
  7.7 5.0 %collective-permute-start = (f32[3,3,96,96]{3,2,1,0:T(8,128)S(1)}, f32[3,3,96,96]{3,2,1,0:T(8,128)S(1)}, u32[]{:S(2)}, u32[]{:S(2)}) collective-permute-start(f32[3,3,96,96]{3,2,1,0:T(8,128)S(1)} %get-tuple-element.9), channel_id=1, source_target_pairs={{0,1},{1,2},{2,3},{4,5},{5,6},{6,7},{8,9},{9,10},{10,11},{12,13},{... | collective-permute-start | bytes 995336 | tf_op jit(solution)/shard_map/ppermute | solution.py:18
  12.7 1.3 collective-permute-start.1
  14.1 2.2 dynamic-slice_bitcast_fusion
  16.3 5.8 %collective-permute-done = f32[3,3,96,96]{3,2,1,0:T(8,128)S(1)} collective-permute-done((f32[3,3,96,96]{3,2,1,0:T(8,128)S(1)}, f32[3,3,96,96]{3,2,1,0:T(8,128)S(1)}, u32[]{:S(2)}, u32[]{:S(2)}) %collective-permute-start) | collective-permute-done | bytes 331808 | tf_op jit(solution)/shard_map/ppermute | solution.py:18
  22.1 4.1 %collective-permute-done.1 = f32[3,3,96,96]{3,2,1,0:T(8,128)S(1)} collective-permute-done((f32[3,3,96,96]{3,2,1,0:T(8,128)S(1)}, f32[3,3,96,96]{3,2,1,0:T(8,128)S(1)}, u32[]{:S(2)}, u32[]{:S(2)}) %collective-permute-start.1) | collective-permute-done | bytes 331808 | tf_op jit(solution)/shard_map/ppermute | solution.py:19
  26.3 0.4 pad_maximum_fusion
  26.7 4.7 %multiply_add_fusion = f32[30,3,96,96]{3,2,1,0:T(8,128)S(1)} fusion(f32[30,3,96,96]{3,2,1,0:T(8,128)S(1)} %pad_maximum_fusion), kind=kLoop, calls=%fused_computation.11 | loop fusion | flops 5806080 | bytes 6635520 | tf_op jit(solution)/shard_map/add | solution.py:29
  31.4 2.7 fusion.3
  34.1 2.4 fusion.10
  36.6 0.3 fusion.20
  37.0 1.9 maximum_maximum_fusion
  38.9 1.0 dynamic-slice_bitcast_fusion.3
  39.9 1.3 collective-permute-start.3
  41.2 4.6 %collective-permute-start.2 = (bf16[1,192,192]{2,1,0:T(8,128)(2,1)S(1)}, bf16[1,192,192]{2,1,0:T(8,128)(2,1)S(1)}, u32[]{:S(2)}, u32[]{:S(2)}) collective-permute-start(bf16[1,192,192]{2,1,0:T(8,128)(2,1)S(1)} %get-tuple-element.6), channel_id=1, source_target_pairs={{0,1},{1,2},{2,3},{4,5},{5,6},{6,7},{8,9},{9,10},{10,11},{12,13},{... | collective-permute-start | bytes 221192 | tf_op jit(solution)/shard_map/ppermute | solution.py:51
  45.8 0.7 dynamic_slice.10
  49.3 0.1 add_convert_fusion
  49.5 0.7 pad_maximum_fusion.2.up_y
  50.2 0.7 pad_maximum_fusion.1.up_x
  51.0 0.8 multiply_convert_fusion
  51.8 0.6 pad_add_fusion.1.sel
  52.4 30.2 %all-gather.3.cloned.1.call-done = bf16[104,3,72,128]{3,2,1,0:T(8,128)(2,1)} async-done(((bf16[26,3,72,128]{3,2,1,0:T(8,128)(2,1)}), bf16[104,3,72,128]{3,2,1,0:T(8,128)(2,1)}) %all-gather.3.cloned.1.call-update) | async-done | bytes 5750800 | tf_op jit(solution)/shard_map/all_gather | solution.py:325
  82.5 38.0 %shard_map.37 = f32[48,288,128]{2,1,0:T(8,128)} custom-call(s32[4]{0:T(128)} %pad_add_fusion.1.sel, bf16[4,26,3,72,128]{4,3,2,1,0:T(8,128)(2,1)} %bitcast.24, bf16[2,48,192,192]{3,2,1,0:T(8,128)(2,1)} %above.1, bf16[2,48,192,192]{3,2,1,0:T(8,128)(2,1)} %above.1, bf16[2,48,192,192]{3,2,1,0:T(8,128)(2,1)} %above.1, bf16[1,192,192]{2,1,0:T(8,128)(2,1)} %copy-done.3, ...), custom_call_target="tpu_custom_call" | custom-call | tf_op jit(solution)/shard_map/pallas_call | solution.py:184
  120.6 112.7 %all-reduce.8.cloned.1.call-done.mean = f32[48,288,128]{2,1,0:T(8,128)} async-done(((f32[48,288,128]{2,1,0:T(8,128)}), f32[48,288,128]{2,1,0:T(8,128)}) %all-reduce.8.cloned.1.call-update) | async-done | bytes 7077904 | tf_op jit(solution)/shard_map/psum | solution.py:331
  233.3 1.1 fusion.19
  234.4 1.3 collective-permute-start.5
  235.7 4.6 %collective-permute-start.4 = (f32[2,288,128]{2,1,0:T(8,128)S(1)}, f32[2,288,128]{2,1,0:T(8,128)S(1)}, u32[]{:S(2)}, u32[]{:S(2)}) collective-permute-start(f32[2,288,128]{2,1,0:T(8,128)S(1)} %get-tuple-element.8), channel_id=1, source_target_pairs={{0,1},{1,2},{2,3},{4,5},{5,6},{6,7},{8,9},{9,10},{10,11},{12,13},{... | collective-permute-start | bytes 884744 | tf_op jit(solution)/shard_map/ppermute | solution.py:51
  240.3 0.7 pad_add_fusion.sel
  240.9 3.8 %collective-permute-done.5.after = f32[2,288,128]{2,1,0:T(8,128)S(1)} collective-permute-done((f32[2,288,128]{2,1,0:T(8,128)S(1)}, f32[2,288,128]{2,1,0:T(8,128)S(1)}, u32[]{:S(2)}, u32[]{:S(2)}) %collective-permute-start.5) | collective-permute-done | bytes 294944 | tf_op jit(solution)/shard_map/ppermute | solution.py:51
  244.8 1.2 collective-permute-done.4.before
  245.9 0.7 copy-done.1
  246.6 25.0 %shard_map.38 = f32[48,192,192]{2,1,0:T(8,128)} custom-call(s32[2]{0:T(128)} %pad_add_fusion.sel, f32[48,288,128]{2,1,0:T(8,128)} %all-reduce.8.cloned.1.call-done.mean, f32[2,288,128]{2,1,0:T(8,128)} %copy-done.1, f32[2,288,128]{2,1,0:T(8,128)} %copy-done), custom_call_target="tpu_custom_call" | custom-call | tf_op jit(solution)/shard_map/pallas_call | solution.py:294
  (25 shorter events, 0.3 us)
Async XLA Ops:
  6.5 76.0 %all-gather.3.cloned.1.call-start = ((), (), s32[]{:S(2)}) async-start(), calls=%async_computation.1 | async-start | bytes 7188480 | tf_op jit(solution)/shard_map/all_gather | solution.py:325
  7.7 14.4 %collective-permute-start = (f32[3,3,96,96]{3,2,1,0:T(8,128)S(1)}, f32[3,3,96,96]{3,2,1,0:T(8,128)S(1)}, u32[]{:S(2)}, u32[]{:S(2)}) collective-permute-start(f32[3,3,96,96]{3,2,1,0:T(8,128)S(1)} %get-tuple-element.9), channel_id=1, source_target_pairs={{0,1},{1,2},{2,3},{4,5},{5,6},{6,7},{8,9},{9,10},{10,11},{12,13},{... | collective-permute-start | bytes 995336 | tf_op jit(solution)/shard_map/ppermute | solution.py:18
  12.7 13.5 %collective-permute-start.1 = (f32[3,3,96,96]{3,2,1,0:T(8,128)S(1)}, f32[3,3,96,96]{3,2,1,0:T(8,128)S(1)}, u32[]{:S(2)}, u32[]{:S(2)}) collective-permute-start(f32[3,3,96,96]{3,2,1,0:T(8,128)S(1)} %get-tuple-element.10), channel_id=1, source_target_pairs={{1,0},{2,1},{3,2},{5,4},{6,5},{7,6},{9,8},{10,9},{11,10},{13,12},{... | collective-permute-start | bytes 995336 | tf_op jit(solution)/shard_map/ppermute | solution.py:19
  36.6 9.1 %copy-start.4 = (s32[8]{0:T(128)S(1)}, s32[8]{0:T(128)}, u32[]{:S(2)}) copy-start(s32[8]{0:T(128)} %param.5) | copy-start | bytes 100
  38.9 194.4 %all-reduce.8.cloned.1.call-start = ((), (), s32[]{:S(2)}) async-start(), calls=%async_computation | async-start | bytes 14155776 | tf_op jit(solution)/shard_map/psum | solution.py:331
  39.9 12.5 %collective-permute-start.3 = (bf16[1,192,192]{2,1,0:T(8,128)(2,1)S(1)}, bf16[1,192,192]{2,1,0:T(8,128)(2,1)S(1)}, u32[]{:S(2)}, u32[]{:S(2)}) collective-permute-start(bf16[1,192,192]{2,1,0:T(8,128)(2,1)S(1)} %get-tuple-element.5), channel_id=1, source_target_pairs={{1,0},{2,1},{3,2},{5,4},{6,5},{7,6},{9,8},{10,9},{11,10},{13,12},{... | collective-permute-start | bytes 221192 | tf_op jit(solution)/shard_map/ppermute | solution.py:51
  41.2 11.2 %collective-permute-start.2 = (bf16[1,192,192]{2,1,0:T(8,128)(2,1)S(1)}, bf16[1,192,192]{2,1,0:T(8,128)(2,1)S(1)}, u32[]{:S(2)}, u32[]{:S(2)}) collective-permute-start(bf16[1,192,192]{2,1,0:T(8,128)(2,1)S(1)} %get-tuple-element.6), channel_id=1, source_target_pairs={{0,1},{1,2},{2,3},{4,5},{5,6},{6,7},{8,9},{9,10},{10,11},{12,13},{... | collective-permute-start | bytes 221192 | tf_op jit(solution)/shard_map/ppermute | solution.py:51
  52.3 30.2 %copy-start.2 = (bf16[1,192,192]{2,1,0:T(8,128)(2,1)}, bf16[1,192,192]{2,1,0:T(8,128)(2,1)S(1)}, u32[]{:S(2)}) copy-start(bf16[1,192,192]{2,1,0:T(8,128)(2,1)S(1)} %collective-permute-done.3.after) | copy-start | bytes 221188
  52.4 30.2 %copy-start.3 = (bf16[1,192,192]{2,1,0:T(8,128)(2,1)}, bf16[1,192,192]{2,1,0:T(8,128)(2,1)S(1)}, u32[]{:S(2)}) copy-start(bf16[1,192,192]{2,1,0:T(8,128)(2,1)S(1)} %collective-permute-done.2.before) | copy-start | bytes 221188
  234.4 10.4 %collective-permute-start.5 = (f32[2,288,128]{2,1,0:T(8,128)S(1)}, f32[2,288,128]{2,1,0:T(8,128)S(1)}, u32[]{:S(2)}, u32[]{:S(2)}) collective-permute-start(f32[2,288,128]{2,1,0:T(8,128)S(1)} %get-tuple-element.7), channel_id=1, source_target_pairs={{1,0},{2,1},{3,2},{5,4},{6,5},{7,6},{9,8},{10,9},{11,10},{13,12},{... | collective-permute-start | bytes 884744 | tf_op jit(solution)/shard_map/ppermute | solution.py:51
  235.7 10.2 %collective-permute-start.4 = (f32[2,288,128]{2,1,0:T(8,128)S(1)}, f32[2,288,128]{2,1,0:T(8,128)S(1)}, u32[]{:S(2)}, u32[]{:S(2)}) collective-permute-start(f32[2,288,128]{2,1,0:T(8,128)S(1)} %get-tuple-element.8), channel_id=1, source_target_pairs={{0,1},{1,2},{2,3},{4,5},{5,6},{6,7},{8,9},{9,10},{10,11},{12,13},{... | collective-permute-start | bytes 884744 | tf_op jit(solution)/shard_map/ppermute | solution.py:51
  244.8 1.2 copy-start
  245.9 0.7 copy-start.1
Sparse Core Ops, SparseCore 0:
  39.0 43.4 all-gather.2
  120.7 112.5 all-reduce.7
where the time goes:
time: 279 us
  waiting for transfers between devices  158 us (57%)
  Pallas kernels  63 us (23%)
  starting transfers between devices  18 us (6%)
  between operations  16.4 us (6%)
  other arithmetic  15.8 us (6%)
  local copies, waits for them, and re-layouts  7.36 us (3%)
    psum x1, waiting for transfers between devices, shards(): mean = lax.psum(total, ('level', 'subj'))  113 us
    pallas_call x1, Pallas kernels, warp(): pl.pallas_call(warp_kernel, grid_spec=grid_spec, out_shape=jax.ShapeDtype...  38 us
    all_gather x1, waiting for transfers between devices, shards(): piece = lax.all_gather(field[None], 'subj', axis=0, tiled=True)  30.2 us
    pallas_call x1, Pallas kernels, sweeps(): pl.pallas_call(sweep_kernel, grid_spec=grid_spec, out_shape=jax.ShapeDtyp...  25 us
    ppermute x4, starting transfers between devices, halo_rows(): return (lax.ppermute(last, axis, up), lax.ppermute(first, axis, down))  11.7 us
    add x2, other arithmetic, band(): (take(0) + take(4)) * 0.0625 + (take(1) + take(3)) * 0.25 + take(2) * 0.375  7.44 us
    ppermute x1, waiting for transfers between devices, with_halo(): before = lax.ppermute(last, axis, up)  5.82 us
  transfers between devices with their start and end apart: 8, of which 6 were waited for; matrix products, arithmetic and copies ran while one was open for 3% of the time, Pallas kernels for 0%

commit v1 on v0

v1 whole, which is shorter than its diff:
```python
import functools

import jax
import jax.numpy as jnp
from jax import lax
from jax.experimental import pallas as pl
from jax.experimental.pallas import tpu as pltpu
from jax.sharding import PartitionSpec as P

LANES = 128
MARGIN = 8
TOP = 32767.0
F32 = jnp.float32
BF16 = jnp.bfloat16


def upsample_table(finest, coarse):
    rows_fine = jnp.arange(finest, dtype=jnp.int32)[:, None]
    columns = jnp.arange(coarse, dtype=jnp.int32)[None, :]
    nearest = rows_fine // 2
    farther = nearest + 2 * (rows_fine % 2) - 1
    return 0.75 * (columns == nearest).astype(F32) + 0.25 * (columns == farther).astype(F32)


def slope_table(finest):
    rows = jnp.arange(finest, dtype=jnp.int32)[:, None]
    columns = jnp.arange(finest, dtype=jnp.int32)[None, :]
    ahead = (columns == rows + 1).astype(F32)
    behind = (columns == rows - 1).astype(F32)
    return ((ahead - behind) * 0.5).astype(BF16)


def blur_table(coarse):
    rows = jnp.arange(coarse, dtype=jnp.int32)[:, None]
    columns = jnp.arange(coarse, dtype=jnp.int32)[None, :]
    gap = jnp.abs(rows - columns)
    return (
        0.375 * (gap == 0).astype(F32)
        + 0.25 * (gap == 1).astype(F32)
        + 0.0625 * (gap == 2).astype(F32)
    ).astype(BF16)


def split(value):
    high = value.astype(BF16)
    low = (value - high.astype(F32)).astype(BF16)
    return jnp.concatenate([high, low], axis=0)


def dot(a, b):
    return jnp.dot(a, b, preferred_element_type=F32)


def encode(packed):
    peak = jnp.max(jnp.abs(packed), axis=0, keepdims=True)
    peak = jnp.maximum(peak, 1e-30)
    code = jnp.floor(packed * (TOP / peak) + 0.5).astype(jnp.int16)
    return code, jnp.broadcast_to(peak * (1.0 / TOP), (8, LANES))


def fused_kernel(
    sel, images, momenta, up_x, up_y, slope_x, slope_y, blur_x, blur_y,
    codes, scales,
    ext, img, vel, fine, part, peer, ycode, yscale, mean, second, packed,
    rescode, resscale, xcode, xscale,
    lsem, hsend, hrecv, vsend, vrecv, psend, precv, ysend, yrecv, msend, mrecv,
    gsend, grecv, xsend, xrecv, osem,
):
    level = lax.axis_index("level")
    group = lax.axis_index("subj")
    zone = lax.axis_index("gz")
    groups = lax.axis_size("subj")
    zones = lax.axis_size("gz")
    chips = groups // 2
    chip = group // 2
    core = group % 2
    partner = 2 * chip + 1 - core
    up = level
    fine_slab, finest = images.shape[1], images.shape[2]
    slab, coarse = momenta.shape[1], momenta.shape[3]
    rows_half, planes_half = slab // 2, fine_slab // 2
    pairs = (rows_half + 2) // 2
    rows_block, planes_block = rows_half // 2, planes_half // 2
    half = finest // 2
    rest = finest - LANES
    piece = LANES - coarse

    to_zone = zone + 1 - 2 * level
    has_to = (to_zone >= 0) & (to_zone < zones)
    from_zone = zone - 1 + 2 * level
    has_from = (from_zone >= 0) & (from_zone < zones)
    far_step = 2 * core - 1
    crosses = level == core
    far_zone = jnp.where(crosses, zone + far_step, zone)
    has_far = (far_zone >= 0) & (far_zone < zones)
    me = (level, group, zone)
    mate = (level, partner, zone)
    across = (1 - level, group, zone)
    far = (1 - level, partner, far_zone)
    upper = (level, group, to_zone)
    lower = (level, group, from_zone)
    peers = [(chip + d) % chips for d in range(1, chips)]

    def remote(src, dst, send, recv, device):
        return pltpu.make_async_remote_copy(
            src_ref=src, dst_ref=dst, send_sem=send, recv_sem=recv,
            device_id=device, device_id_type=pl.DeviceIdType.MESH,
        )

    load_mom = pltpu.make_async_copy(
        momenta.at[:, pl.ds(level * (rows_half - 3), rows_half + 3)],
        ext.at[:, pl.ds(3 - 3 * level, rows_half + 3)],
        lsem.at[0],
    )
    load_img = pltpu.make_async_copy(
        images.at[:, pl.ds(level * (planes_half - 1), planes_half + 1)],
        img.at[:, pl.ds(1 - level, planes_half + 1)],
        lsem.at[1],
    )
    load_mom.start()
    load_img.start()
    zero_plane = jnp.zeros(mean.shape[1:], F32)

    def clear(j, _):
        mean[j] = zero_plane
        second[j] = zero_plane
        return 0

    lax.fori_loop(0, planes_block + 4, clear, 0)

    barrier = pltpu.get_barrier_semaphore()

    def greet(device):
        pl.semaphore_signal(
            barrier, inc=1, device_id=device, device_id_type=pl.DeviceIdType.MESH
        )

    greet(mate)
    greet(across)
    for other in peers:
        greet((level, 2 * other + core, zone))

    @pl.when(has_to)
    def _():
        greet(upper)

    @pl.when(has_from)
    def _():
        greet(lower)

    @pl.when(has_far)
    def _():
        greet(far)

    pl.semaphore_wait(
        barrier,
        2 + len(peers)
        + has_to.astype(jnp.int32) + has_from.astype(jnp.int32) + has_far.astype(jnp.int32),
    )

    halo_mom = remote(
        momenta.at[:, pl.ds((1 - level) * (slab - 3), 3)],
        ext.at[:, pl.ds(level * (rows_half + 3), 3)],
        hsend.at[0], hrecv.at[0], upper,
    )
    halo_img = remote(
        images.at[:, pl.ds((1 - level) * (fine_slab - 1), 1)],
        img.at[:, pl.ds(level * (planes_half + 1), 1)],
        hsend.at[1], hrecv.at[1], upper,
    )

    @pl.when(has_to)
    def _():
        halo_mom.start()
        halo_img.start()

    @pl.when(jnp.logical_not(has_from))
    def _():
        for s in range(2):
            for e in range(3):
                for k in range(3):
                    ext[s, level * (rows_half + 3) + e, k] = jnp.zeros((coarse, coarse), F32)
            img[s, level * (planes_half + 1)] = jnp.zeros((finest, finest), BF16)

    load_mom.wait()

    def pair_of(i):
        return i + (1 - up) * (pairs - 1 - 2 * i)

    lane = lax.broadcasted_iota(jnp.int32, (coarse, LANES), 1)

    def velocity_sends(t):
        sends = [
            remote(
                vel.at[t, group], vel.at[t, group], vsend.at[t, 0], vrecv.at[t, group], mate
            )
        ]
        for n, other in enumerate(peers):
            sends.append(
                remote(
                    vel.at[t, group], vel.at[t, group], vsend.at[t, 1 + n],
                    vrecv.at[t, group], (level, 2 * other + core, zone),
                )
            )
        return sends

    def relay_sends(t):
        sends = []
        for n, other in enumerate(peers):
            there = 2 * other + core
            sends.append(
                remote(
                    vel.at[t, there], vel.at[t, there], vsend.at[t, chips + n],
                    vrecv.at[t, there], mate,
                )
            )
        return sends

    def smooth(i, _):
        t = pair_of(i)

        @pl.when((i == pairs - 2) & has_from)
        def _():
            halo_mom.wait_recv()

        planes = {}
        for r in range(2):
            row = zone * slab + level * rows_half - 1 + 2 * t + r
            keep = ((row >= 0) & (row < slab * zones)).astype(F32)
            for s in range(2):
                for k in range(3):
                    f = [ext[s, 2 * t + r + o, k] for o in range(5)]
                    value = (f[0] + f[4]) * 0.0625 + (f[1] + f[3]) * 0.25 + f[2] * 0.375
                    wide = dot(split(value), blur_x[...])
                    wide = (wide[:coarse] + wide[coarse:]) * keep
                    planes[6 * r + 3 * s + k] = dot(blur_y[...], split(wide))
        for m in range(3):
            for j in range(3):
                turned = pltpu.roll(planes[9 + m], coarse - piece * j, 1)
                joined = jnp.where(lane < coarse, planes[3 * m + j], turned)
                vel[t, group, 3 * m + j] = joined.astype(BF16)

        @pl.when(i > 0)
        def _():
            for send in velocity_sends(pair_of(i - 1)):
                send.start()

        return 0

    lax.fori_loop(0, pairs, smooth, 0)
    for send in velocity_sends(pair_of(pairs - 1)):
        send.start()

    load_img.wait()

    @pl.when(has_from)
    def _():
        halo_img.wait_recv()

    def relay(t):
        for send in relay_sends(t):
            send.wait_recv()
            send.start()

    def pick(t, source, first, count):
        value = vel[t, 0, first : first + count]
        for other in range(1, groups):
            value = jnp.where(source == other, vel[t, other, first : first + count], value)
        return value

    def raise_row(t, r, s, source):
        slot = lax.rem(2 * t + r, 4)
        if 6 * r + 3 * s < 9:
            chosen = pick(t, source, 6 * r + 3 * s, 3).reshape(3 * coarse, LANES)
            wide = dot(chosen, up_x[0])
            parts = [wide[coarse * k : coarse * (k + 1)] for k in range(3)]
        else:
            chosen = pick(t, source, 0, 9)
            parts = []
            for k in range(3):
                total = dot(chosen[3 * k], up_x[1])
                for j in range(1, 3):
                    total = total + dot(chosen[3 * k + j], up_x[1 + j])
                parts.append(total)
        for k in range(3):
            fine[s, slot, k] = dot(up_y[...], split(parts[k]))

    chunk = finest // 4

    def warp_plane(row, z):
        middle = lax.rem(row, 4)
        outer = lax.rem(row + 3 + 2 * z, 4)
        plane = 2 * (row - 1) + z
        for r in range(0, finest, chunk):
            rows = pl.ds(r, chunk)
            total = None
            for s in range(2):
                image = img[s, plane + 1, rows, :]
                dx = dot(image, slope_x[...])
                dy = dot(slope_y[rows, :], img[s, plane + 1])
                back = img[s, plane, rows, :].astype(F32)
                ahead = img[s, plane + 2, rows, :].astype(F32)
                dz = (ahead - back) * 0.5
                near = (
                    fine[s, middle, 0, rows, :] * dx
                    + fine[s, middle, 1, rows, :] * dy
                    + fine[s, middle, 2, rows, :] * dz
                )
                side = (
                    fine[s, outer, 0, rows, :] * dx
                    + fine[s, outer, 1, rows, :] * dy
                    + fine[s, outer, 2, rows, :] * dz
                )
                value = image.astype(F32) - (0.75 * near + 0.25 * side)
                total = value if total is None else total + value
            part[plane, rows, :] = total[:, :LANES]
            place = rest * (r // half)
            part[plane, pl.ds(finest + r % half, chunk), place : place + rest] = total[:, LANES:]

    def chip_send(row):
        here = lax.rem(row, rows_block)
        return remote(
            part.at[pl.ds(2 * row, 2)], peer.at[pl.ds(2 * here, 2)],
            psend.at[here], precv.at[here], mate,
        )

    def sum_sends(here):
        sends = []
        for n, other in enumerate(peers):
            there = (level, 2 * other + core, zone)
            at = pl.ds(2 * here, 2)
            sends.append(
                remote(
                    ycode.at[chip, at], ycode.at[chip, at], ysend.at[0, here, n],
                    yrecv.at[0, here, chip], there,
                )
            )
            sends.append(
                remote(
                    yscale.at[chip, at], yscale.at[chip, at], ysend.at[1, here, n],
                    yrecv.at[1, here, chip], there,
                )
            )
        return sends

    def settle(row):
        here = lax.rem(row, rows_block)
        chip_send(row).wait_recv()
        for z in range(2):
            code, scale = encode(part[2 * row + z] + peer[2 * here + z])
            ycode[chip, 2 * here + z] = code
            yscale[chip, 2 * here + z] = scale
        for send in sum_sends(here):
            send.start()

    def row_at(n):
        return n + (1 - up) * (rows_half - 1 - 2 * n)

    def owned(row):
        return (row // rows_block) == core

    relay(pair_of(0))

    def main(i, _):
        t = pair_of(i)
        for other in range(chips):
            theirs = 2 * other + 1 - core
            remote(
                vel.at[t, theirs], vel.at[t, theirs], vsend.at[t, 0], vrecv.at[t, theirs], mate
            ).wait_recv()
        for r in range(2):
            for s in range(2):
                raise_row(t, r, s, sel[s])

        @pl.when(i < pairs - 1)
        def _():
            relay(pair_of(i + 1))

        @pl.when(i >= 1)
        def _():
            def step(w, _):
                n = 2 * (i - 1) + w // 2
                row = row_at(n)
                warp_plane(row + 1, lax.rem(w, 2))

                @pl.when(lax.rem(w, 2) == 1)
                def _():
                    @pl.when(jnp.logical_not(owned(row)))
                    def _():
                        chip_send(row).start()

                    prior = row_at(jnp.maximum(n - 1, 0))

                    @pl.when((n > 0) & owned(prior))
                    def _():
                        settle(prior)

                return 0

            lax.fori_loop(0, 4, step, 0)

        return 0

    lax.fori_loop(0, pairs, main, 0)
    final_row = row_at(rows_half - 1)

    @pl.when(owned(final_row))
    def _():
        settle(final_row)

    subjects = 2 * groups

    def enter(n, _):
        here = n + (1 - up) * (rows_block - 1 - 2 * n)
        at = pl.ds(2 * here, 2)
        for other in peers:
            remote(
                ycode.at[other, at], ycode.at[other, at], ysend.at[0, here, 0],
                yrecv.at[0, here, other], me,
            ).wait_recv()
            remote(
                yscale.at[other, at], yscale.at[other, at], ysend.at[1, here, 0],
                yrecv.at[1, here, other], me,
            ).wait_recv()
        for z in range(2):
            plane = 2 * here + z
            value = ycode[0, plane].astype(F32) * yscale[0, plane][:1]
            for other in range(1, chips):
                value = value + ycode[other, plane].astype(F32) * yscale[other, plane][:1]
            value = value * (1.0 / subjects)
            mean[2 + plane, pl.ds(MARGIN, finest), 0:LANES] = value[:finest]
            side = value[finest:]
            mean[2 + plane, pl.ds(MARGIN, half), LANES:finest] = side[:, :rest]
            turned = pltpu.roll(side, LANES - rest, 1)
            mean[2 + plane, pl.ds(MARGIN + half, half), LANES:finest] = turned[:, :rest]
        return 0

    lax.fori_loop(0, rows_block, enter, 0)

    inner_from = 2 + core * 0 + (1 - core) * (planes_block - 2)
    inner_to = core * 0 + (1 - core) * 0 + core * (planes_block + 2)
    outer_from = 2 + core * (planes_block - 2)
    outer_to = (1 - core) * (planes_block + 2)
    edge_mate = remote(
        mean.at[pl.ds(inner_from, 2)], mean.at[pl.ds(inner_to, 2)],
        msend.at[0], mrecv.at[0], mate,
    )
    edge_far = remote(
        mean.at[pl.ds(outer_from, 2)], mean.at[pl.ds(outer_to, 2)],
        msend.at[1], mrecv.at[1], far,
    )

    @pl.when(has_far)
    def _():
        edge_far.start()

    edge_mate.start()
    edge_mate.wait_recv()

    @pl.when(has_far)
    def _():
        edge_far.wait_recv()

    step_rows = finest // 3

    def relax(ref, slot, r):
        rows = pl.ds(MARGIN + r, step_rows)
        center = ref[slot, rows, :]
        width = center.shape[1]
        neighbours = (
            ref[slot - 1, rows, :]
            + ref[slot + 1, rows, :]
            + ref[slot, pl.ds(MARGIN + r - 1, step_rows), :]
            + ref[slot, pl.ds(MARGIN + r + 1, step_rows), :]
            + pltpu.roll(center, 1, 1)
            + pltpu.roll(center, width - 1, 1)
        )
        return center + 0.15 * (neighbours - 6.0 * center)

    low_edge = (core == 0) & jnp.logical_not(has_far)
    high_edge = (core == 1) & jnp.logical_not(has_far)

    def first_sweep(j, _):
        drop = ((j == 1) & low_edge) | ((j == planes_block + 2) & high_edge)
        keep = jnp.where(drop, 0.0, 1.0)
        for r in range(0, finest, step_rows):
            value = relax(mean, j, r) * keep
            second[j, pl.ds(MARGIN + r, step_rows), 0:finest] = value[:, :finest]
        return 0

    lax.fori_loop(1, planes_block + 3, first_sweep, 0)

    base = (2 * level + core) * planes_block
    away = (2 * (1 - level) + core) * planes_block

    def result_sends(j):
        at = pl.ds(j, 1)
        out = codes.at[pl.ds(base + j, 1)]
        return [
            remote(rescode.at[at], xcode.at[at], xsend.at[j], xrecv.at[j], across),
            remote(rescode.at[at], out, gsend.at[0, j], grecv.at[0, j], mate),
            pltpu.make_async_copy(rescode.at[at], out, osem.at[0, j]),
        ]

    def second_sweep(j, _):
        parts = []
        for r in range(0, finest, step_rows):
            value = relax(second, j + 2, r)
            packed[pl.ds(r, step_rows), :] = value[:, :LANES]
            parts.append(value[:, LANES:finest])
        side = jnp.concatenate(parts, axis=0)
        packed[pl.ds(finest, half), 0:rest] = side[:half]
        packed[pl.ds(finest, half), rest:LANES] = side[half:]
        code, scale = encode(packed[...])
        rescode[j] = code
        resscale[j] = scale

        @pl.when(j > 0)
        def _():
            for send in result_sends(j - 1):
                send.start()

        return 0

    lax.fori_loop(0, planes_block, second_sweep, 0)
    for send in result_sends(planes_block - 1):
        send.start()
    scale_out = scales.at[pl.ds(base, planes_block)]
    scale_sends = [
        remote(resscale, xscale, xsend.at[planes_block], xrecv.at[planes_block], across),
        remote(resscale, scale_out, gsend.at[0, planes_block], grecv.at[0, planes_block], mate),
        pltpu.make_async_copy(resscale, scale_out, osem.at[0, planes_block]),
    ]
    for send in scale_sends:
        send.start()

    def hand_sends(j):
        at = pl.ds(j, 1)
        out = codes.at[pl.ds(away + j, 1)]
        return [
            remote(xcode.at[at], out, gsend.at[1, j], grecv.at[1, j], mate),
            pltpu.make_async_copy(xcode.at[at], out, osem.at[1, j]),
        ]

    def hand(j, _):
        result_sends(j)[0].wait_recv()
        for send in hand_sends(j):
            send.start()
        return 0

    lax.fori_loop(0, planes_block, hand, 0)
    scale_away = scales.at[pl.ds(away, planes_block)]
    scale_hands = [
        remote(xscale, scale_away, gsend.at[1, planes_block], grecv.at[1, planes_block], mate),
        pltpu.make_async_copy(xscale, scale_away, osem.at[1, planes_block]),
    ]
    scale_sends[0].wait_recv()
    for send in scale_hands:
        send.start()

    @pl.when(has_to)
    def _():
        halo_mom.wait_send()
        halo_img.wait_send()

    def drain_velocity(t, _):
        for send in velocity_sends(t) + relay_sends(t):
            send.wait_send()
        return 0

    lax.fori_loop(0, pairs, drain_velocity, 0)

    def drain_rows(here, _):
        chip_send((1 - core) * rows_block + here).wait_send()
        for send in sum_sends(here):
            send.wait_send()
        return 0

    lax.fori_loop(0, rows_block, drain_rows, 0)
    edge_mate.wait_send()

    @pl.when(has_far)
    def _():
        edge_far.wait_send()

    def drain_results(j, _):
        cross, over, local = result_sends(j)
        cross.wait_send()
        over.wait()
        local.wait()
        over, local = hand_sends(j)
        over.wait()
        local.wait()
        return 0

    lax.fori_loop(0, planes_block, drain_results, 0)
    scale_sends[0].wait_send()
    scale_sends[1].wait()
    scale_sends[2].wait()
    scale_hands[0].wait()
    scale_hands[1].wait()


def fused(sel, images, momenta):
    groups = lax.axis_size("subj")
    chips = groups // 2
    fine_slab, finest = images.shape[1], images.shape[2]
    slab, coarse = momenta.shape[1], momenta.shape[3]
    rows_half, planes_half = slab // 2, fine_slab // 2
    pairs = (rows_half + 2) // 2
    rows_block, planes_block = rows_half // 2, planes_half // 2
    tall = finest + finest // 2
    piece = LANES - coarse
    table = upsample_table(finest, coarse).astype(BF16)
    columns = table.T
    up_x = [jnp.pad(columns, ((0, piece), (0, 0)))]
    for i in range(0, coarse, piece):
        up_x.append(jnp.pad(columns[i : i + piece], ((coarse, 0), (0, 0))))
    up_x = jnp.stack(up_x)
    up_y = jnp.concatenate([table, table], axis=1)
    slope = slope_table(finest)
    blur = blur_table(coarse)
    blur_x = jnp.pad(blur, ((0, 0), (0, piece)))
    blur_y = jnp.concatenate([blur, blur], axis=1)
    width = -(-(finest + 1) // LANES) * LANES
    dma = pltpu.SemaphoreType.DMA
    vmem = pl.BlockSpec(memory_space=pltpu.VMEM)
    hbm = pl.BlockSpec(memory_space=pl.ANY)
    volume = (planes_block + 4, finest + 2 * MARGIN, width)
    scratch = [
        pltpu.VMEM((2, rows_half + 6, 3, coarse, coarse), F32),
        pltpu.VMEM((2, planes_half + 2, finest, finest), BF16),
        pltpu.VMEM((pairs, groups, 9, coarse, LANES), BF16),
        pltpu.VMEM((2, 4, 3, finest, finest), F32),
        pltpu.VMEM((planes_half, tall, LANES), F32),
        pltpu.VMEM((planes_block, tall, LANES), F32),
        pltpu.VMEM((chips, planes_block, tall, LANES), jnp.int16),
        pltpu.VMEM((chips, planes_block, 8, LANES), F32),
        pltpu.VMEM(volume, F32),
        pltpu.VMEM(volume, F32),
        pltpu.VMEM((tall, LANES), F32),
        pltpu.VMEM((planes_block, tall, LANES), jnp.int16),
        pltpu.VMEM((planes_block, 8, LANES), F32),
        pltpu.VMEM((planes_block, tall, LANES), jnp.int16),
        pltpu.VMEM((planes_block, 8, LANES), F32),
        dma((2,)),
        dma((2,)),
        dma((2,)),
        dma((pairs, 2 * chips)),
        dma((pairs, groups)),
        dma((rows_block,)),
        dma((rows_block,)),
        dma((2, rows_block, max(chips - 1, 1))),
        dma((2, rows_block, chips)),
        dma((2,)),
        dma((2,)),
        dma((2, planes_block + 1)),
        dma((2, planes_block + 1)),
        dma((planes_block + 1,)),
        dma((planes_block + 1,)),
        dma((2, planes_block + 1)),
    ]
    return pl.pallas_call(
        fused_kernel,
        out_shape=(
            jax.ShapeDtypeStruct((fine_slab, tall, LANES), jnp.int16),
            jax.ShapeDtypeStruct((fine_slab, 8, LANES), F32),
        ),
        in_specs=[pl.BlockSpec(memory_space=pltpu.SMEM), hbm, hbm] + [vmem] * 6,
        out_specs=(hbm, hbm),
        scratch_shapes=scratch,
        compiler_params=pltpu.CompilerParams(
            collective_id=0, has_side_effects=True, vmem_limit_bytes=60 * 1024 * 1024
        ),
    )(sel, images, momenta, up_x, up_y, slope.T, slope, blur_x, blur_y)


def decode_kernel(codes, scales, out):
    finest = out.shape[1]
    half = finest // 2
    rest = finest - LANES
    for z in range(out.shape[0]):
        value = codes[z].astype(F32) * scales[z][:1]
        out[z, :, 0:LANES] = value[:finest]
        side = value[finest:]
        out[z, 0:half, LANES:finest] = side[:, :rest]
        turned = pltpu.roll(side, LANES - rest, 1)
        out[z, half:finest, LANES:finest] = turned[:, :rest]


def decode(codes, scales, finest):
    planes, tall = codes.shape[0], codes.shape[1]
    block = 4
    return pl.pallas_call(
        decode_kernel,
        grid=(planes // block,),
        in_specs=[
            pl.BlockSpec((block, tall, LANES), lambda j: (j, 0, 0)),
            pl.BlockSpec((block, 8, LANES), lambda j: (j, 0, 0)),
        ],
        out_specs=pl.BlockSpec((block, finest, finest), lambda j: (j, 0, 0)),
        out_shape=jax.ShapeDtypeStruct((planes, finest, finest), F32),
        compiler_params=pltpu.CompilerParams(dimension_semantics=("arbitrary",)),
    )(codes, scales)


def shards(images, momenta, assign):
    count = momenta.shape[0]
    group = lax.axis_index("subj")
    sel = lax.dynamic_slice_in_dim(assign, group * count, count, 0) // count
    codes, scales = fused(sel.astype(jnp.int32), images, momenta)
    return decode(codes, scales, images.shape[2])


def solution(mesh):
    return jax.shard_map(
        shards,
        mesh=mesh,
        in_specs=(P("subj", "gz", None, None), P("subj", "gz", None, None, None), P()),
        out_specs=P("gz", None, None),
        check_vma=False,
    )
```

time: 279 us -> 113 us (0.41)
  waiting for transfers between devices: 158 us -> 0 us
  Pallas kernels: 63 us -> 108 us
  starting transfers between devices: 18 us -> 0 us
  between operations: 16.4 us -> 0.05 us
  other arithmetic: 15.8 us -> 4.45 us
  local copies, waits for them, and re-layouts: 7.36 us -> 0.65 us
    psum x1 -> x0, waiting for transfers between devices: 113 us -> none  [shards(): mean = lax.psum(total, ('level', 'subj'))]
    pallas_call x2, Pallas kernels: 63 us -> 108 us  [the longest x1 98.1 us: fused(): pl.pallas_call(fused_kernel, out_shape=(jax.ShapeDtypeStruct((fine_slab,...]
    all_gather x1 -> x0, waiting for transfers between devices: 30.2 us -> none  [shards(): piece = lax.all_gather(field[None], 'subj', axis=0, tiled=True)]
    ppermute x6 -> x0, starting transfers between devices: 18 us -> none  [the longest x4 11.7 us: halo_rows(): return (lax.ppermute(last, axis, up), lax.ppermute(first, axis, down))]
    ppermute x6 -> x0, waiting for transfers between devices: 15 us -> none  [the longest x1 5.82 us: with_halo(): before = lax.ppermute(last, axis, up)]
    add x2 -> x0, other arithmetic: 7.44 us -> none  [band(): (take(0) + take(4)) * 0.0625 + (take(1) + take(3)) * 0.25 + take(2) * 0.375]
    squeeze x2 -> x0, local copies, waits for them, and re-layouts: 3.2 us -> none  [the longest x1 2.24 us: shards(): moment = lax.dynamic_index_in_dim(momenta, ticker, 0, keepdims=False)]
  transfers between devices with their start and end apart: 8 -> 0, of which waited for: 6 -> 0; matrix products, arithmetic and copies ran while one was open for 3% -> 0% of each run, Pallas kernels for 0% -> 0%
where the time goes in v1:
time: 113 us
  Pallas kernels  108 us (96%)
  other arithmetic  4.45 us (4%)
    pallas_call x1, Pallas kernels, fused(): pl.pallas_call(fused_kernel, out_shape=(jax.ShapeDtypeStruct((fine_slab,...  98.1 us
    pallas_call x1, Pallas kernels, decode(): pl.pallas_call(decode_kernel, grid=(planes // block,), in_specs=[pl.Block...  9.52 us

profile of v1, /device:TPU:0, one launch (start us, length us, event | category | flops | bytes accessed | tf_op | source)
XLA Modules:
  0.0 112.7 jit_solution(8768504565700713162)
XLA Ops:
  0.0 1.3 %and_select_fusion.2.sel = s32[2]{0:T(128)} fusion(s32[8]{0:T(128)} %param.5, s32[]{:T(128)S(6)} %select_n.53), kind=kLoop, calls=%fused_computation.29 | loop fusion | flops 30 | bytes 20 | tf_op jit(solution)/shard_map/jit(floor_divide)/jit(_where)/select_n | solution.py:710
  1.3 0.6 pad.22.blur_x
  1.9 0.7 pad_maximum_fusion.2.blur_y
  2.6 0.1 add_convert_fusion
  2.8 0.7 pad_maximum_fusion.1.up_y
  3.5 0.8 pad_maximum_fusion.up_x
  4.3 0.8 multiply_convert_fusion
  5.1 98.1 %shard_map.37 = (s16[48,288,128]{2,1,0:T(8,128)(2,1)}, f32[48,8,128]{2,1,0:T(8,128)}) custom-call(s32[2]{0:T(128)} %and_select_fusion.2.sel, bf16[2,48,192,192]{3,2,1,0:T(8,128)(2,1)} %images.1, f32[2,24,3,96,96]{4,3,2,1,0:T(8,128)} %momenta.1, bf16[4,128,192]{2,1,0:T(8,128)(2,1)} %pad_maximum_fusion.up_x, bf16[192,192]{1,0:T(8,128)(2,1)} %pad_maximum_fusion.1.up_y, ...), custom_call_target="tpu_custom_call" | custom-call | tf_op jit(solution)/shard_map/pallas_call | solution.py:663
  103.2 9.5 %shard_map.38 = f32[48,192,192]{2,1,0:T(8,128)} custom-call(s16[48,288,128]{2,1,0:T(8,128)(2,1)} %get-tuple-element.7.codes, f32[48,8,128]{2,1,0:T(8,128)} %get-tuple-element.8.scales), custom_call_target="tpu_custom_call" | custom-call | tf_op jit(solution)/shard_map/pallas_call | solution.py:694
  (9 shorter events, 0.1 us)

commit v2 on v1

v2 whole, which is shorter than its diff:
```python
import functools

import jax
import jax.numpy as jnp
from jax import lax
from jax.experimental import pallas as pl
from jax.experimental.pallas import tpu as pltpu
from jax.sharding import PartitionSpec as P

LANES = 128
MARGIN = 8
TOP = 32767.0
F32 = jnp.float32
BF16 = jnp.bfloat16


def split(value):
    high = value.astype(BF16)
    low = (value - high.astype(F32)).astype(BF16)
    return jnp.concatenate([high, low], axis=0)


def dot(a, b):
    return jnp.dot(a, b, preferred_element_type=F32)


def encode(packed):
    peak = jnp.max(jnp.abs(packed), axis=0, keepdims=True)
    peak = jnp.maximum(peak, 1e-30)
    code = jnp.floor(packed * (TOP / peak) + 0.5).astype(jnp.int16)
    return code, jnp.broadcast_to(peak * (1.0 / TOP), (8, LANES))


def iota(shape, axis):
    return lax.broadcasted_iota(jnp.int32, shape, axis)


def weight(fine_index, coarse_index, coarse):
    nearest = jnp.right_shift(fine_index, 1)
    farther = nearest + 2 * jnp.bitwise_and(fine_index, 1) - 1
    value = jnp.where(coarse_index == nearest, 0.75, jnp.where(coarse_index == farther, 0.25, 0.0))
    return jnp.where((coarse_index >= 0) & (coarse_index < coarse), value, 0.0).astype(BF16)


def slope(ahead, behind):
    return jnp.where(ahead, 0.5, jnp.where(behind, -0.5, 0.0)).astype(BF16)


def blur(gap):
    value = jnp.where(gap == 1, 0.25, jnp.where(gap == 2, 0.0625, 0.0))
    return jnp.where(gap == 0, 0.375, value).astype(BF16)


def make_tables(up_x, up_y, slope_x, slope_y, blur_x, blur_y):
    finest = up_y.shape[0]
    coarse = blur_x.shape[0]
    piece = LANES - coarse
    shape = (LANES, finest)
    lane, column = iota(shape, 0), iota(shape, 1)
    up_x[0] = weight(column, lane, coarse)
    for j in range(up_x.shape[0] - 1):
        index = jnp.where(lane >= coarse, lane - coarse + piece * j, -1)
        up_x[1 + j] = weight(column, index, coarse)
    shape = up_y.shape
    row, column = iota(shape, 0), iota(shape, 1)
    up_y[...] = weight(row, jnp.where(column >= coarse, column - coarse, column), coarse)
    slope_y[...] = slope(column == row + 1, column == row - 1)
    slope_x[...] = slope(row == column + 1, row == column - 1)
    shape = blur_x.shape
    blur_x[...] = jnp.where(
        iota(shape, 1) < coarse, blur(jnp.abs(iota(shape, 0) - iota(shape, 1))), 0.0
    ).astype(BF16)
    shape = blur_y.shape
    column = iota(shape, 1)
    column = jnp.where(column >= coarse, column - coarse, column)
    blur_y[...] = blur(jnp.abs(iota(shape, 0) - column))


def fused_kernel(
    assign, images, momenta,
    codes, scales,
    up_x, up_y, slope_x, slope_y, blur_x, blur_y,
    ext, img, vel, fine, part, peer, ycode, yscale, mcode, mscale, xcode, xscale,
    lsem, hsend, hrecv, vsend, vrecv, psend, precv, ysend, yrecv,
    gsend, grecv, xsend, xrecv, osem, zsend, zrecv,
):
    level = lax.axis_index("level")
    group = lax.axis_index("subj")
    zone = lax.axis_index("gz")
    groups = lax.axis_size("subj")
    zones = lax.axis_size("gz")
    chips = groups // 2
    chip = group // 2
    core = group % 2
    partner = 2 * chip + 1 - core
    up = level
    fine_slab, finest = images.shape[1], images.shape[2]
    slab, coarse = momenta.shape[1], momenta.shape[3]
    rows_half, planes_half = slab // 2, fine_slab // 2
    pairs = (rows_half + 2) // 2
    rows_block, planes_block = rows_half // 2, planes_half // 2
    half = finest // 2
    rest = finest - LANES
    piece = LANES - coarse

    to_zone = zone + 1 - 2 * level
    has_to = (to_zone >= 0) & (to_zone < zones)
    from_zone = zone - 1 + 2 * level
    has_from = (from_zone >= 0) & (from_zone < zones)
    me = (level, group, zone)
    mate = (level, partner, zone)
    across = (1 - level, group, zone)
    upper = (level, group, to_zone)
    peers = [(chip + d) % chips for d in range(1, chips)]

    def remote(src, dst, send, recv, device):
        return pltpu.make_async_remote_copy(
            src_ref=src, dst_ref=dst, send_sem=send, recv_sem=recv,
            device_id=device, device_id_type=pl.DeviceIdType.MESH,
        )

    load_mom = pltpu.make_async_copy(
        momenta.at[:, pl.ds(level * (rows_half - 3), rows_half + 3)],
        ext.at[:, pl.ds(3 - 3 * level, rows_half + 3)],
        lsem.at[0],
    )
    load_img = pltpu.make_async_copy(
        images.at[:, pl.ds(level * (planes_half - 1), planes_half + 1)],
        img.at[:, pl.ds(1 - level, planes_half + 1)],
        lsem.at[1],
    )
    load_mom.start()
    load_img.start()
    barrier = pltpu.get_barrier_semaphore()

    def greet(device):
        pl.semaphore_signal(
            barrier, inc=1, device_id=device, device_id_type=pl.DeviceIdType.MESH
        )

    block = [(a, 2 * chip + b) for a in range(2) for b in range(2)]
    for a, b in block:
        @pl.when((a != level) | (b != group))
        def _(a=a, b=b):
            greet((a, b, zone))

    for other in peers:
        greet((level, 2 * other + core, zone))
    has_before = zone > 0
    has_after = zone < zones - 1

    @pl.when(has_before)
    def _():
        for a, b in block:
            greet((a, b, zone - 1))

    @pl.when(has_after)
    def _():
        for a, b in block:
            greet((a, b, zone + 1))

    make_tables(up_x, up_y, slope_x, slope_y, blur_x, blur_y)
    pl.semaphore_wait(
        barrier,
        3 + len(peers)
        + 4 * has_before.astype(jnp.int32) + 4 * has_after.astype(jnp.int32),
    )

    halo_mom = remote(
        momenta.at[:, pl.ds((1 - level) * (slab - 3), 3)],
        ext.at[:, pl.ds(level * (rows_half + 3), 3)],
        hsend.at[0], hrecv.at[0], upper,
    )
    halo_img = remote(
        images.at[:, pl.ds((1 - level) * (fine_slab - 1), 1)],
        img.at[:, pl.ds(level * (planes_half + 1), 1)],
        hsend.at[1], hrecv.at[1], upper,
    )

    @pl.when(has_to)
    def _():
        halo_mom.start()
        halo_img.start()

    @pl.when(jnp.logical_not(has_from))
    def _():
        for s in range(2):
            for e in range(3):
                for k in range(3):
                    ext[s, level * (rows_half + 3) + e, k] = jnp.zeros((coarse, coarse), F32)
            img[s, level * (planes_half + 1)] = jnp.zeros((finest, finest), BF16)

    load_mom.wait()

    def pair_of(i):
        return i + (1 - up) * (pairs - 1 - 2 * i)

    lane = lax.broadcasted_iota(jnp.int32, (coarse, LANES), 1)

    def velocity_sends(t):
        sends = [
            remote(
                vel.at[t, group], vel.at[t, group], vsend.at[t, 0], vrecv.at[t, group], mate
            )
        ]
        for n, other in enumerate(peers):
            sends.append(
                remote(
                    vel.at[t, group], vel.at[t, group], vsend.at[t, 1 + n],
                    vrecv.at[t, group], (level, 2 * other + core, zone),
                )
            )
        return sends

    def relay_sends(t):
        sends = []
        for n, other in enumerate(peers):
            there = 2 * other + core
            sends.append(
                remote(
                    vel.at[t, there], vel.at[t, there], vsend.at[t, chips + n],
                    vrecv.at[t, there], mate,
                )
            )
        return sends

    def smooth(i):
        t = pair_of(i)
        planes = {}
        for r in range(2):
            row = zone * slab + level * rows_half - 1 + 2 * t + r
            keep = ((row >= 0) & (row < slab * zones)).astype(F32)
            for s in range(2):
                for k in range(3):
                    f = [ext[s, 2 * t + r + o, k] for o in range(5)]
                    value = (f[0] + f[4]) * 0.0625 + (f[1] + f[3]) * 0.25 + f[2] * 0.375
                    wide = dot(split(value), blur_x[...])
                    wide = (wide[:coarse] + wide[coarse:]) * keep
                    planes[6 * r + 3 * s + k] = dot(blur_y[...], split(wide))
        for m in range(3):
            for j in range(3):
                turned = pltpu.roll(planes[9 + m], coarse - piece * j, 1)
                joined = jnp.where(lane < coarse, planes[3 * m + j], turned)
                vel[t, group, 3 * m + j] = joined.astype(BF16)

    def share(i):
        for send in velocity_sends(pair_of(i)):
            send.start()

    def begin(i, _):
        smooth(i)

        @pl.when(i > 0)
        def _():
            share(i - 1)

        return 0

    lax.fori_loop(0, pairs - 2, begin, 0)
    share(pairs - 3)

    load_img.wait()

    def relay(t):
        for send in relay_sends(t):
            send.wait_recv()
            send.start()

    def pick(t, source, first, count):
        value = vel[t, 0, first : first + count]
        for other in range(1, groups):
            value = jnp.where(source[other], vel[t, other, first : first + count], value)
        return value

    def raise_row(t, r, s, source):
        slot = lax.rem(2 * t + r, 4)
        if 6 * r + 3 * s < 9:
            chosen = pick(t, source, 6 * r + 3 * s, 3).reshape(3 * coarse, LANES)
            wide = dot(chosen, up_x[0])
            parts = [wide[coarse * k : coarse * (k + 1)] for k in range(3)]
        else:
            chosen = pick(t, source, 0, 9)
            parts = []
            for k in range(3):
                total = dot(chosen[3 * k], up_x[1])
                for j in range(1, 3):
                    total = total + dot(chosen[3 * k + j], up_x[1 + j])
                parts.append(total)
        for k in range(3):
            fine[s, slot, k] = dot(up_y[...], split(parts[k]))

    chunk = finest // 4

    def warp_plane(row, z):
        middle = lax.rem(row, 4)
        outer = lax.rem(row + 3 + 2 * z, 4)
        plane = 2 * (row - 1) + z
        for r in range(0, finest, chunk):
            rows = pl.ds(r, chunk)
            total = None
            for s in range(2):
                image = img[s, plane + 1, rows, :]
                dx = dot(image, slope_x[...])
                dy = dot(slope_y[rows, :], img[s, plane + 1])
                back = img[s, plane, rows, :].astype(F32)
                ahead = img[s, plane + 2, rows, :].astype(F32)
                dz = (ahead - back) * 0.5
                near = (
                    fine[s, middle, 0, rows, :] * dx
                    + fine[s, middle, 1, rows, :] * dy
                    + fine[s, middle, 2, rows, :] * dz
                )
                side = (
                    fine[s, outer, 0, rows, :] * dx
                    + fine[s, outer, 1, rows, :] * dy
                    + fine[s, outer, 2, rows, :] * dz
                )
                value = image.astype(F32) - (0.75 * near + 0.25 * side)
                total = value if total is None else total + value
            part[plane, rows, :] = total[:, :LANES]
            place = rest * (r // half)
            part[plane, pl.ds(finest + r % half, chunk), place : place + rest] = total[:, LANES:]

    def chip_send(row):
        here = lax.rem(row, rows_block)
        return remote(
            part.at[pl.ds(2 * row, 2)], peer.at[pl.ds(2 * here, 2)],
            psend.at[here], precv.at[here], mate,
        )

    def sum_sends(here):
        sends = []
        for n, other in enumerate(peers):
            there = (level, 2 * other + core, zone)
            at = pl.ds(2 * here, 2)
            sends.append(
                remote(
                    ycode.at[chip, at], ycode.at[chip, at], ysend.at[0, here, n],
                    yrecv.at[0, here, chip], there,
                )
            )
            sends.append(
                remote(
                    yscale.at[chip, at], yscale.at[chip, at], ysend.at[1, here, n],
                    yrecv.at[1, here, chip], there,
                )
            )
        return sends

    def settle(row):
        here = lax.rem(row, rows_block)
        chip_send(row).wait_recv()
        for z in range(2):
            code, scale = encode(part[2 * row + z] + peer[2 * here + z])
            ycode[chip, 2 * here + z] = code
            yscale[chip, 2 * here + z] = scale
        for send in sum_sends(here):
            send.start()

    def row_at(n):
        return n + (1 - up) * (rows_half - 1 - 2 * n)

    def owned(row):
        return (row // rows_block) == core

    subjects = 2 * groups
    base = 2 + (2 * level + core) * planes_block
    away = 2 + (2 * (1 - level) + core) * planes_block

    def block_row(n):
        return n + (1 - up) * (rows_block - 1 - 2 * n)

    def spread(here):
        at = pl.ds(2 * here, 2)
        out = pl.ds(base + 2 * here, 2)
        sends = []
        for n, (src, cross, dst) in enumerate(((mcode, xcode, codes), (mscale, xscale, scales))):
            sends += [
                remote(src.at[at], cross.at[at], xsend.at[n, here], xrecv.at[n, here], across),
                remote(src.at[at], dst.at[out], gsend.at[n, 0, here], grecv.at[n, 0, here], mate),
                pltpu.make_async_copy(src.at[at], dst.at[out], osem.at[n, 0, here]),
            ]
        return sends

    def hand_on(here):
        at = pl.ds(2 * here, 2)
        out = pl.ds(away + 2 * here, 2)
        sends = []
        for n, (src, dst) in enumerate(((xcode, codes), (xscale, scales))):
            sends += [
                remote(src.at[at], dst.at[out], gsend.at[n, 1, here], grecv.at[n, 1, here], mate),
                pltpu.make_async_copy(src.at[at], dst.at[out], osem.at[n, 1, here]),
            ]
        return sends

    outermost = (level == core) & has_from
    edge_at = pl.ds(level * 2 * (rows_block - 1), 2)
    edge_out = pl.ds((1 - level) * (fine_slab + 2), 2)

    def edge_sends():
        sends = []
        for m, (a, b) in enumerate(block):
            for n, (src, dst) in enumerate(((mcode, codes), (mscale, scales))):
                sends.append(
                    remote(
                        src.at[edge_at], dst.at[edge_out], zsend.at[n, m],
                        zrecv.at[n, 1 - level], (a, b, from_zone),
                    )
                )
        return sends

    def publish(here):
        at = pl.ds(2 * here, 2)
        for other in peers:
            for n, buffer in enumerate((ycode, yscale)):
                remote(
                    buffer.at[other, at], buffer.at[other, at], ysend.at[n, here, 0],
                    yrecv.at[n, here, other], me,
                ).wait_recv()
        for z in range(2):
            plane = 2 * here + z
            value = ycode[0, plane].astype(F32) * yscale[0, plane][:1]
            for other in range(1, chips):
                value = value + ycode[other, plane].astype(F32) * yscale[other, plane][:1]
            code, scale = encode(value * (1.0 / subjects))
            mcode[plane] = code
            mscale[plane] = scale
        for send in spread(here):
            send.start()

    is_first = core == 1 - up
    early = min(4, rows_block)
    halo_at = (pairs - 3) // 2
    sources = []
    for s in range(2):
        row = assign[2 * group + s]
        sources.append([row == 2 * other + s for other in range(groups)])

    relay(pair_of(0))

    def main(i, _):
        t = pair_of(i)

        @pl.when((i == halo_at) & has_from)
        def _():
            halo_mom.wait_recv()

        late = (i == halo_at) | (i == halo_at + 1)
        late_pair = pairs - 2 + i - halo_at

        @pl.when(late)
        def _():
            smooth(late_pair)

        for other in range(chips):
            theirs = 2 * other + 1 - core
            remote(
                vel.at[t, theirs], vel.at[t, theirs], vsend.at[t, 0], vrecv.at[t, theirs], mate
            ).wait_recv()
        for r in range(2):
            for s in range(2):
                raise_row(t, r, s, sources[s])

        @pl.when(late)
        def _():
            share(late_pair)

        @pl.when(i < pairs - 1)
        def _():
            relay(pair_of(i + 1))

        @pl.when((i == pairs - 1) & has_from)
        def _():
            halo_img.wait_recv()

        @pl.when(i >= 1)
        def _():
            def step(w, _):
                n = 2 * (i - 1) + w // 2
                row = row_at(n)
                warp_plane(row + 1, lax.rem(w, 2))

                @pl.when(lax.rem(w, 2) == 1)
                def _():
                    @pl.when(jnp.logical_not(owned(row)))
                    def _():
                        chip_send(row).start()

                    prior = row_at(jnp.maximum(n - 1, 0))

                    @pl.when((n > 0) & owned(prior))
                    def _():
                        settle(prior)

                @pl.when((i == pairs - 1) & is_first & (w < early))
                def _():
                    publish(block_row(w))

                return 0

            lax.fori_loop(0, 4, step, 0)

        return 0

    lax.fori_loop(0, pairs, main, 0)

    @pl.when(jnp.logical_not(is_first))
    def _():
        settle(row_at(rows_half - 1))

    def finish(n, _):
        @pl.when(jnp.logical_not(is_first) | (n >= early))
        def _():
            publish(block_row(n))

        return 0

    lax.fori_loop(0, rows_block, finish, 0)

    @pl.when(outermost)
    def _():
        for send in edge_sends():
            send.start()

    def hand(n, _):
        here = rows_block - 1 - block_row(n)
        first, second = spread(here)[0], spread(here)[3]
        first.wait_recv()
        second.wait_recv()
        for send in hand_on(here):
            send.start()
        return 0

    lax.fori_loop(0, rows_block, hand, 0)

    @pl.when(has_to)
    def _():
        halo_mom.wait_send()
        halo_img.wait_send()

    def drain_velocity(t, _):
        for send in velocity_sends(t) + relay_sends(t):
            send.wait_send()
        return 0

    lax.fori_loop(0, pairs, drain_velocity, 0)

    def drain_rows(here, _):
        chip_send((1 - core) * rows_block + here).wait_send()
        for send in sum_sends(here):
            send.wait_send()
        for n, send in enumerate(spread(here)):
            if n % 3 == 0:
                send.wait_send()
            else:
                send.wait()
        for send in hand_on(here):
            send.wait()
        return 0

    lax.fori_loop(0, rows_block, drain_rows, 0)

    @pl.when(outermost)
    def _():
        for send in edge_sends():
            send.wait_send()

    for side, there in ((0, has_before), (1, has_after)):
        @pl.when(there)
        def _(side=side):
            out = pl.ds(side * (fine_slab + 2), 2)
            for n, dst in enumerate((codes, scales)):
                remote(dst.at[out], dst.at[out], zsend.at[n, 0], zrecv.at[n, side], me).wait_recv()


def fused(assign, images, momenta):
    groups = lax.axis_size("subj")
    chips = groups // 2
    fine_slab, finest = images.shape[1], images.shape[2]
    slab, coarse = momenta.shape[1], momenta.shape[3]
    rows_half, planes_half = slab // 2, fine_slab // 2
    pairs = (rows_half + 2) // 2
    rows_block, planes_block = rows_half // 2, planes_half // 2
    tall = finest + finest // 2
    tables = 1 + coarse // (LANES - coarse)
    dma = pltpu.SemaphoreType.DMA
    hbm = pl.BlockSpec(memory_space=pl.ANY)
    scratch = [
        pltpu.VMEM((tables, LANES, finest), BF16),
        pltpu.VMEM((finest, finest), BF16),
        pltpu.VMEM((finest, finest), BF16),
        pltpu.VMEM((finest, finest), BF16),
        pltpu.VMEM((coarse, LANES), BF16),
        pltpu.VMEM((coarse, 2 * coarse), BF16),
        pltpu.VMEM((2, rows_half + 6, 3, coarse, coarse), F32),
        pltpu.VMEM((2, planes_half + 2, finest, finest), BF16),
        pltpu.VMEM((pairs, groups, 9, coarse, LANES), BF16),
        pltpu.VMEM((2, 4, 3, finest, finest), F32),
        pltpu.VMEM((planes_half, tall, LANES), F32),
        pltpu.VMEM((planes_block, tall, LANES), F32),
        pltpu.VMEM((chips, planes_block, tall, LANES), jnp.int16),
        pltpu.VMEM((chips, planes_block, 8, LANES), F32),
        pltpu.VMEM((planes_block, tall, LANES), jnp.int16),
        pltpu.VMEM((planes_block, 8, LANES), F32),
        pltpu.VMEM((planes_block, tall, LANES), jnp.int16),
        pltpu.VMEM((planes_block, 8, LANES), F32),
        dma((2,)),
        dma((2,)),
        dma((2,)),
        dma((pairs, 2 * chips)),
        dma((pairs, groups)),
        dma((rows_block,)),
        dma((rows_block,)),
        dma((2, rows_block, max(chips - 1, 1))),
        dma((2, rows_block, chips)),
        dma((2, 2, rows_block)),
        dma((2, 2, rows_block)),
        dma((2, rows_block)),
        dma((2, rows_block)),
        dma((2, 2, rows_block)),
        dma((2, 4)),
        dma((2, 2)),
    ]
    return pl.pallas_call(
        fused_kernel,
        out_shape=(
            jax.ShapeDtypeStruct((fine_slab + 4, tall, LANES), jnp.int16),
            jax.ShapeDtypeStruct((fine_slab + 4, 8, LANES), F32),
        ),
        in_specs=[pl.BlockSpec(memory_space=pltpu.SMEM), hbm, hbm],
        out_specs=(hbm, hbm),
        scratch_shapes=scratch,
        compiler_params=pltpu.CompilerParams(
            collective_id=0, has_side_effects=True, vmem_limit_bytes=60 * 1024 * 1024
        ),
    )(assign, images, momenta)


STEP = 4
RING = 8


def sweep_kernel(codes, scales, out, first, second):
    step = pl.program_id(0)
    last = pl.num_programs(0) - 1
    zone = lax.axis_index("gz")
    zones = lax.axis_size("gz")
    finest = out.shape[1]
    half = finest // 2
    rest = finest - LANES
    wide_at = MARGIN
    tail_at = finest + 3 * MARGIN
    base = STEP * lax.rem(step, 2)
    lane = iota((half, LANES), 1)
    edge = iota((MARGIN, LANES), 1)
    low = zone == 0
    high = zone == zones - 1

    def slot(o):
        return lax.rem(base + o + RING, RING)

    def put(ref, at, top, bottom, tail):
        ref[at, pl.ds(wide_at, half), :] = top
        ref[at, pl.ds(wide_at + half, half), :] = bottom
        ref[at, pl.ds(tail_at, half), :] = tail
        above = pltpu.roll(tail[half - MARGIN :], LANES - rest, 1)
        below = pltpu.roll(tail[:MARGIN], LANES - rest, 1)
        ref[at, pl.ds(tail_at - MARGIN, MARGIN), :] = jnp.where(edge >= rest, above, 0.0)
        ref[at, pl.ds(tail_at + half, MARGIN), :] = jnp.where(edge < rest, below, 0.0)

    def around(ref, o, at, center):
        rows = pl.ds(at, half)
        here = slot(o)
        return (
            ref[slot(o - 1), rows, :]
            + ref[slot(o + 1), rows, :]
            + ref[here, pl.ds(at - 1, half), :]
            + ref[here, pl.ds(at + 1, half), :]
        )

    def relax(ref, o):
        here = slot(o)
        top = ref[here, pl.ds(wide_at, half), :]
        bottom = ref[here, pl.ds(wide_at + half, half), :]
        tail = ref[here, pl.ds(tail_at, half), :]
        top_west = pltpu.roll(top, 1, 1)
        bottom_west = pltpu.roll(bottom, 1, 1)
        tail_east = pltpu.roll(tail, LANES - 1, 1)
        total = around(ref, o, wide_at, top)
        total = total + jnp.where(lane == 0, 0.0, top_west)
        total = total + jnp.where(lane == LANES - 1, tail_east, pltpu.roll(top, LANES - 1, 1))
        new_top = 0.1 * top + 0.15 * total
        total = around(ref, o, wide_at + half, bottom)
        total = total + jnp.where(lane == 0, 0.0, bottom_west)
        total = total + jnp.where(
            lane == LANES - 1, pltpu.roll(tail, rest - 1, 1), pltpu.roll(bottom, LANES - 1, 1)
        )
        new_bottom = 0.1 * bottom + 0.15 * total
        total = around(ref, o, tail_at, tail)
        west = jnp.where(lane == 0, top_west, pltpu.roll(tail, 1, 1))
        total = total + jnp.where(lane == rest, pltpu.roll(bottom, rest + 1, 1), west)
        ends = (lane == rest - 1) | (lane == LANES - 1)
        total = total + jnp.where(ends, 0.0, tail_east)
        new_tail = 0.1 * tail + 0.15 * total
        return new_top, new_bottom, new_tail

    @pl.when(step == 0)
    def _():
        first[...] = jnp.zeros_like(first)
        second[...] = jnp.zeros_like(second)

    for o in range(STEP):
        value = codes[o].astype(F32) * scales[o][:1]
        if o < 2:
            value = jnp.where((step == 0) & low, 0.0, value)
        else:
            value = jnp.where((step == last) & high, 0.0, value)
        put(first, slot(o), value[:half], value[half:finest], value[finest:])

    for o in range(-1, STEP - 1):
        parts = relax(first, o)
        if o == 1:
            parts = [jnp.where((step == 0) & low, 0.0, p) for p in parts]
        if o == 2:
            parts = [jnp.where((step == last) & high, 0.0, p) for p in parts]
        put(second, slot(o), *parts)

    @pl.when(step >= 1)
    def _():
        for o in range(-2, STEP - 2):
            top, bottom, tail = relax(second, o)
            out[o + 2, 0:half, 0:LANES] = top
            out[o + 2, half:finest, 0:LANES] = bottom
            out[o + 2, 0:half, LANES:finest] = tail[:, :rest]
            out[o + 2, half:finest, LANES:finest] = pltpu.roll(tail, rest, 1)[:, :rest]


def sweeps(codes, scales, finest):
    planes, tall = codes.shape[0] - 4, codes.shape[1]
    ring = pltpu.VMEM((RING, tall + 4 * MARGIN, LANES), F32)
    return pl.pallas_call(
        sweep_kernel,
        grid=(planes // STEP + 1,),
        in_specs=[
            pl.BlockSpec((STEP, tall, LANES), lambda j: (j, 0, 0)),
            pl.BlockSpec((STEP, 8, LANES), lambda j: (j, 0, 0)),
        ],
        out_specs=pl.BlockSpec(
            (STEP, finest, finest), lambda j: (jnp.maximum(j - 1, 0), 0, 0)
        ),
        out_shape=jax.ShapeDtypeStruct((planes, finest, finest), F32),
        scratch_shapes=[ring, ring],
        compiler_params=pltpu.CompilerParams(dimension_semantics=("arbitrary",)),
    )(codes, scales)


def shards(images, momenta, assign):
    codes, scales = fused(assign, images, momenta)
    return sweeps(codes, scales, images.shape[2])


def solution(mesh):
    return jax.shard_map(
        shards,
        mesh=mesh,
        in_specs=(P("subj", "gz", None, None), P("subj", "gz", None, None, None), P()),
        out_specs=P("gz", None, None),
        check_vma=False,
    )
```

time: 113 us -> 102 us (0.903); the launches traced: 113 us -> 100 us
  Pallas kernels: 108 us -> 100 us
  other arithmetic: 4.45 us -> 0 us
    pallas_call x2, Pallas kernels: 108 us -> 100 us  [the longest x1 79.5 us: fused(): pl.pallas_call(fused_kernel, out_shape=(jax.ShapeDtypeStruct((fine_slab +...]
    concatenate x2 -> x0, other arithmetic: 1.43 us -> none  [the longest x1 0.73 us: fused(): up_y = jnp.concatenate([table, table], axis=1)]
    select_n x2 -> x0, other arithmetic: 1.26 us -> none  [the longest x1 1.25 us: shards(): sel = lax.dynamic_slice_in_dim(assign, group * count, count, 0) // count]
where the time goes in v2:
time: 102 us; the launch traced here: 100 us
  Pallas kernels  100 us (98%)
    pallas_call x1, Pallas kernels, fused(): pl.pallas_call(fused_kernel, out_shape=(jax.ShapeDtypeStruct((fine_slab +...  79.5 us
    pallas_call x1, Pallas kernels, sweeps(): pl.pallas_call(sweep_kernel, grid=(planes // STEP + 1,), in_specs=[pl.Blo...  20.7 us

profile of v2, /device:TPU:0, one launch (start us, length us, event | category | flops | bytes accessed | tf_op | source)
XLA Modules:
  0.0 100.2 jit_solution(17989211751327069062)
XLA Ops:
  0.0 79.5 %shard_map.37 = (s16[52,288,128]{2,1,0:T(8,128)(2,1)}, f32[52,8,128]{2,1,0:T(8,128)}) custom-call(s32[8]{0:T(128)} %assign.1, bf16[2,48,192,192]{3,2,1,0:T(8,128)(2,1)} %images.1, f32[2,24,3,96,96]{4,3,2,1,0:T(8,128)} %momenta.1), custom_call_target="tpu_custom_call" | custom-call | tf_op jit(solution)/shard_map/pallas_call | solution.py:624
  79.5 20.7 %shard_map.38 = f32[48,192,192]{2,1,0:T(8,128)} custom-call(s16[52,288,128]{2,1,0:T(8,128)(2,1)} %get-tuple-element.7.codes, f32[52,8,128]{2,1,0:T(8,128)} %get-tuple-element.8.scales), custom_call_target="tpu_custom_call" | custom-call | tf_op jit(solution)/shard_map/pallas_call | solution.py:741

commit v3 on v2

--- a/solution.py
+++ b/solution.py
@@ -10,6 +10,7 @@
 LANES = 128
 MARGIN = 8
 TOP = 32767.0
+LIMIT = 18.0
 F32 = jnp.float32
 BF16 = jnp.bfloat16
 
@@ -77,11 +78,11 @@
 
 
 def fused_kernel(
-    assign, images, momenta,
+    messages, assign, images, momenta,
     codes, scales,
     up_x, up_y, slope_x, slope_y, blur_x, blur_y,
-    ext, img, vel, fine, part, peer, ycode, yscale, mcode, mscale, xcode, xscale,
-    lsem, hsend, hrecv, vsend, vrecv, psend, precv, ysend, yrecv,
+    ext, edges, hout, hin, img, vel, ymsg, fine, part, peer, ycode, yscale, mcode, mscale, xcode, xscale,
+    lsem, hsend, hrecv, vsend, vrecv, qsend, qrecv, psend, precv, ysend, yrecv,
     gsend, grecv, xsend, xrecv, osem, zsend, zrecv,
 ):
     level = lax.axis_index("level")
@@ -129,8 +130,11 @@
         img.at[:, pl.ds(1 - level, planes_half + 1)],
         lsem.at[1],
     )
+    load_edges = pltpu.make_async_copy(
+        momenta.at[:, pl.ds((1 - level) * (slab - 3), 3)], edges, lsem.at[2]
+    )
+    load_edges.start()
     load_mom.start()
-    load_img.start()
     barrier = pltpu.get_barrier_semaphore()
 
     def greet(device):
@@ -160,17 +164,19 @@
             greet((a, b, zone + 1))
 
     make_tables(up_x, up_y, slope_x, slope_y, blur_x, blur_y)
+    load_edges.wait()
+    for s in range(2):
+        for e in range(3):
+            for k in range(3):
+                code = jnp.floor(edges[s, e, k] * (TOP / LIMIT) + 0.5)
+                hout[s, e, k] = jnp.clip(code, -TOP, TOP).astype(jnp.int16)
     pl.semaphore_wait(
         barrier,
         3 + len(peers)
         + 4 * has_before.astype(jnp.int32) + 4 * has_after.astype(jnp.int32),
     )
 
-    halo_mom = remote(
-        momenta.at[:, pl.ds((1 - level) * (slab - 3), 3)],
-        ext.at[:, pl.ds(level * (rows_half + 3), 3)],
-        hsend.at[0], hrecv.at[0], upper,
-    )
+    halo_mom = remote(hout, hin, hsend.at[0], hrecv.at[0], upper)
     halo_img = remote(
         images.at[:, pl.ds((1 - level) * (fine_slab - 1), 1)],
         img.at[:, pl.ds(level * (planes_half + 1), 1)],
@@ -191,38 +197,80 @@
             img[s, level * (planes_half + 1)] = jnp.zeros((finest, finest), BF16)
 
     load_mom.wait()
+    load_img.start()
 
     def pair_of(i):
         return i + (1 - up) * (pairs - 1 - 2 * i)
 
-    lane = lax.broadcasted_iota(jnp.int32, (coarse, LANES), 1)
-
-    def velocity_sends(t):
-        sends = [
+    strip = coarse // 2
+    lane = iota((strip, LANES), 1)
+
+    sources = [assign[2 * group + s] for s in range(2)]
+    pieces = [(s, c) for s in range(2) for c in range(2)]
+
+    def ranks(home):
+        count = jnp.int32(0)
+        places = {}
+        for s, c in pieces:
+            needed = jnp.bool_(False)
+            for d in range(1, chips):
+                there = (home + d) % chips
+                for b in range(2):
+                    row = assign[2 * (2 * there + b) + s]
+                    needed = needed | (row == 2 * (2 * home + c) + s)
+            places[s, c] = (needed, count)
+            count = count + needed.astype(jnp.int32)
+        return places
+
+    def near_flag(s, c):
+        return sources[s] == 2 * (2 * chip + c) + s
+
+    if messages == 1:
+        mine = ranks(chip)
+        theirs_of = {other: ranks(peer_chip) for other, peer_chip in enumerate(peers)}
+
+    def item_flag(s, other, n):
+        if messages == 2:
+            if n // 2 != s:
+                return None
+            return sources[s] == 2 * (2 * peers[other] + n % 2) + s
+        flag = jnp.bool_(False)
+        for c in range(2):
+            needed, place = theirs_of[other][s, c]
+            here = sources[s] == 2 * (2 * peers[other] + c) + s
+            flag = flag | (here & needed & (place == n))
+        return flag
+
+    def near_send(t):
+        return remote(vel.at[t, core], vel.at[t, core], vsend.at[t], vrecv.at[t], mate)
+
+    def message_sends(t):
+        part_of = ymsg.at[t, chip, :, pl.ds(strip * core, strip)]
+        return [
             remote(
-                vel.at[t, group], vel.at[t, group], vsend.at[t, 0], vrecv.at[t, group], mate
+                part_of, part_of, qsend.at[t, n], qrecv.at[t, chip, core],
+                (level, 2 * other + core, zone),
             )
+            for n, other in enumerate(peers)
         ]
+
+    def relay_sends(t):
+        sends = []
         for n, other in enumerate(peers):
+            part_of = ymsg.at[t, other, :, pl.ds(strip * core, strip)]
             sends.append(
                 remote(
-                    vel.at[t, group], vel.at[t, group], vsend.at[t, 1 + n],
-                    vrecv.at[t, group], (level, 2 * other + core, zone),
+                    part_of, part_of, qsend.at[t, chips - 1 + n], qrecv.at[t, other, core], mate
                 )
             )
         return sends
 
-    def relay_sends(t):
-        sends = []
-        for n, other in enumerate(peers):
-            there = 2 * other + core
-            sends.append(
-                remote(
-                    vel.at[t, there], vel.at[t, there], vsend.at[t, chips + n],
-                    vrecv.at[t, there], mate,
-                )
-            )
-        return sends
+    def await_relayed(t):
+        for other in peers:
+            part_of = ymsg.at[t, other, :, pl.ds(strip * (1 - core), strip)]
+            remote(
+                part_of, part_of, qsend.at[t, 0], qrecv.at[t, other, 1 - core], mate
+            ).wait_recv()
 
     def smooth(i):
         t = pair_of(i)
@@ -237,18 +285,45 @@
                     wide = dot(split(value), blur_x[...])
                     wide = (wide[:coarse] + wide[coarse:]) * keep
                     planes[6 * r + 3 * s + k] = dot(blur_y[...], split(wide))
-        for m in range(3):
-            for j in range(3):
-                turned = pltpu.roll(planes[9 + m], coarse - piece * j, 1)
-                joined = jnp.where(lane < coarse, planes[3 * m + j], turned)
-                vel[t, group, 3 * m + j] = joined.astype(BF16)
+        for p in range(12):
+            vel[t, core, p] = planes[p].astype(BF16)
+
+    def compose(t):
+        rows = pl.ds(strip * core, strip)
+        for m in range(messages):
+            planes = []
+            for r in range(2):
+                for n in (2 * m, 2 * m + 1):
+                    for k in range(3):
+                        if messages == 2:
+                            value = vel[t, n % 2, 6 * r + 3 * (n // 2) + k, rows]
+                        else:
+                            value = vel[t, 0, 6 * r + k, rows]
+                            for s, c in pieces[1:]:
+                                needed, place = mine[s, c]
+                                value = jnp.where(
+                                    needed & (place == n),
+                                    vel[t, c, 6 * r + 3 * s + k, rows],
+                                    value,
+                                )
+                        planes.append(value)
+            for a in range(3):
+                extra = planes[9 + a].astype(F32)
+                for j in range(3):
+                    turned = pltpu.roll(extra, coarse - piece * j, 1)
+                    joined = jnp.where(lane < coarse, planes[3 * a + j].astype(F32), turned)
+                    ymsg[t, chip, 9 * m + 3 * a + j, rows] = joined.astype(BF16)
 
     def share(i):
-        for send in velocity_sends(pair_of(i)):
+        t = pair_of(i)
+        near_send(t).wait_recv()
+        compose(t)
+        for send in message_sends(t):
             send.start()
 
     def begin(i, _):
         smooth(i)
+        near_send(pair_of(i)).start()
 
         @pl.when(i > 0)
         def _():
@@ -266,28 +341,36 @@
             send.wait_recv()
             send.start()
 
-    def pick(t, source, first, count):
-        value = vel[t, 0, first : first + count]
-        for other in range(1, groups):
-            value = jnp.where(source[other], vel[t, other, first : first + count], value)
-        return value
-
-    def raise_row(t, r, s, source):
+    def raise_row(t, r, s):
         slot = lax.rem(2 * t + r, 4)
-        if 6 * r + 3 * s < 9:
-            chosen = pick(t, source, 6 * r + 3 * s, 3).reshape(3 * coarse, LANES)
-            wide = dot(chosen, up_x[0])
-            parts = [wide[coarse * k : coarse * (k + 1)] for k in range(3)]
-        else:
-            chosen = pick(t, source, 0, 9)
-            parts = []
-            for k in range(3):
-                total = dot(chosen[3 * k], up_x[1])
+        p = 6 * r + 3 * s
+        value = jnp.where(near_flag(s, 1), vel[t, 1, p : p + 3], vel[t, 0, p : p + 3])
+        spread_out, spread_flag = None, jnp.bool_(False)
+        for other in range(len(peers)):
+            for n in range(2 * messages):
+                flag = item_flag(s, other, n)
+                if flag is None:
+                    continue
+                first = 9 * (n // 2)
+                if r == 0 or n % 2 == 0:
+                    at = first + 6 * r + 3 * (n % 2)
+                    value = jnp.where(flag, ymsg[t, peers[other], at : at + 3], value)
+                else:
+                    group_of = ymsg[t, peers[other], first : first + 9]
+                    if spread_out is None:
+                        spread_out = group_of
+                    else:
+                        spread_out = jnp.where(flag, group_of, spread_out)
+                    spread_flag = spread_flag | flag
+        wide = dot(value.reshape(3 * coarse, LANES), up_x[0])
+        for k in range(3):
+            part_of = wide[coarse * k : coarse * (k + 1)]
+            if spread_out is not None:
+                total = dot(spread_out[3 * k], up_x[1])
                 for j in range(1, 3):
-                    total = total + dot(chosen[3 * k + j], up_x[1 + j])
-                parts.append(total)
-        for k in range(3):
-            fine[s, slot, k] = dot(up_y[...], split(parts[k]))
+                    total = total + dot(spread_out[3 * k + j], up_x[1 + j])
+                part_of = jnp.where(spread_flag, total, part_of)
+            fine[s, slot, k] = dot(up_y[...], split(part_of))
 
     chunk = finest // 4
 
@@ -431,11 +514,6 @@
     is_first = core == 1 - up
     early = min(4, rows_block)
     halo_at = (pairs - 3) // 2
-    sources = []
-    for s in range(2):
-        row = assign[2 * group + s]
-        sources.append([row == 2 * other + s for other in range(groups)])
-
     relay(pair_of(0))
 
     def main(i, _):
@@ -444,6 +522,11 @@
         @pl.when((i == halo_at) & has_from)
         def _():
             halo_mom.wait_recv()
+            for s in range(2):
+                for e in range(3):
+                    for k in range(3):
+                        value = hin[s, e, k].astype(F32) * (LIMIT / TOP)
+                        ext[s, level * (rows_half + 3) + e, k] = value
 
         late = (i == halo_at) | (i == halo_at + 1)
         late_pair = pairs - 2 + i - halo_at
@@ -451,23 +534,20 @@
         @pl.when(late)
         def _():
             smooth(late_pair)
-
-        for other in range(chips):
-            theirs = 2 * other + 1 - core
-            remote(
-                vel.at[t, theirs], vel.at[t, theirs], vsend.at[t, 0], vrecv.at[t, theirs], mate
-            ).wait_recv()
+            near_send(pair_of(late_pair)).start()
+
+        @pl.when(i < pairs - 1)
+        def _():
+            relay(pair_of(i + 1))
+
+        await_relayed(t)
         for r in range(2):
             for s in range(2):
-                raise_row(t, r, s, sources[s])
+                raise_row(t, r, s)
 
         @pl.when(late)
         def _():
             share(late_pair)
-
-        @pl.when(i < pairs - 1)
-        def _():
-            relay(pair_of(i + 1))
 
         @pl.when((i == pairs - 1) & has_from)
         def _():
@@ -539,7 +619,8 @@
         halo_img.wait_send()
 
     def drain_velocity(t, _):
-        for send in velocity_sends(t) + relay_sends(t):
+        near_send(t).wait_send()
+        for send in message_sends(t) + relay_sends(t):
             send.wait_send()
         return 0
 
@@ -573,7 +654,7 @@
                 remote(dst.at[out], dst.at[out], zsend.at[n, 0], zrecv.at[n, side], me).wait_recv()
 
 
-def fused(assign, images, momenta):
+def fused(messages, assign, images, momenta):
     groups = lax.axis_size("subj")
     chips = groups // 2
     fine_slab, finest = images.shape[1], images.shape[2]
@@ -593,8 +674,12 @@
         pltpu.VMEM((coarse, LANES), BF16),
         pltpu.VMEM((coarse, 2 * coarse), BF16),
         pltpu.VMEM((2, rows_half + 6, 3, coarse, coarse), F32),
+        pltpu.VMEM((2, 3, 3, coarse, coarse), F32),
+        pltpu.VMEM((2, 3, 3, coarse, coarse), jnp.int16),
+        pltpu.VMEM((2, 3, 3, coarse, coarse), jnp.int16),
         pltpu.VMEM((2, planes_half + 2, finest, finest), BF16),
-        pltpu.VMEM((pairs, groups, 9, coarse, LANES), BF16),
+        pltpu.VMEM((pairs, 2, 12, coarse, LANES), BF16),
+        pltpu.VMEM((pairs, chips, 9 * messages, coarse, LANES), BF16),
         pltpu.VMEM((2, 4, 3, finest, finest), F32),
         pltpu.VMEM((planes_half, tall, LANES), F32),
         pltpu.VMEM((planes_block, tall, LANES), F32),
@@ -604,11 +689,13 @@
         pltpu.VMEM((planes_block, 8, LANES), F32),
         pltpu.VMEM((planes_block, tall, LANES), jnp.int16),
         pltpu.VMEM((planes_block, 8, LANES), F32),
+        dma((3,)),
         dma((2,)),
         dma((2,)),
-        dma((2,)),
-        dma((pairs, 2 * chips)),
-        dma((pairs, groups)),
+        dma((pairs,)),
+        dma((pairs,)),
+        dma((pairs, 2 * (chips - 1))),
+        dma((pairs, chips, 2)),
         dma((rows_block,)),
         dma((rows_block,)),
         dma((2, rows_block, max(chips - 1, 1))),
@@ -622,7 +709,7 @@
         dma((2, 2)),
     ]
     return pl.pallas_call(
-        fused_kernel,
+        functools.partial(fused_kernel, messages),
         out_shape=(
             jax.ShapeDtypeStruct((fine_slab + 4, tall, LANES), jnp.int16),
             jax.ShapeDtypeStruct((fine_slab + 4, 8, LANES), F32),
@@ -631,7 +718,7 @@
         out_specs=(hbm, hbm),
         scratch_shapes=scratch,
         compiler_params=pltpu.CompilerParams(
-            collective_id=0, has_side_effects=True, vmem_limit_bytes=60 * 1024 * 1024
+            collective_id=messages, has_side_effects=True, vmem_limit_bytes=60 * 1024 * 1024
         ),
     )(assign, images, momenta)
 
@@ -640,7 +727,7 @@
 RING = 8
 
 
-def sweep_kernel(codes, scales, out, first, second):
+def sweep_kernel(codes, scales, out, first, second, first_x, second_x, link, cross):
     step = pl.program_id(0)
     last = pl.num_programs(0) - 1
     zone = lax.axis_index("gz")
@@ -651,88 +738,100 @@
     wide_at = MARGIN
     tail_at = finest + 3 * MARGIN
     base = STEP * lax.rem(step, 2)
-    lane = iota((half, LANES), 1)
+    piece = half // 3
     edge = iota((MARGIN, LANES), 1)
-    low = zone == 0
-    high = zone == zones - 1
+    low_first = (step == 0) & (zone == 0)
+    high_last = (step == last) & (zone == zones - 1)
 
     def slot(o):
         return lax.rem(base + o + RING, RING)
 
-    def put(ref, at, top, bottom, tail):
-        ref[at, pl.ds(wide_at, half), :] = top
-        ref[at, pl.ds(wide_at + half, half), :] = bottom
-        ref[at, pl.ds(tail_at, half), :] = tail
-        above = pltpu.roll(tail[half - MARGIN :], LANES - rest, 1)
-        below = pltpu.roll(tail[:MARGIN], LANES - rest, 1)
-        ref[at, pl.ds(tail_at - MARGIN, MARGIN), :] = jnp.where(edge >= rest, above, 0.0)
-        ref[at, pl.ds(tail_at + half, MARGIN), :] = jnp.where(edge < rest, below, 0.0)
-
-    def around(ref, o, at, center):
-        rows = pl.ds(at, half)
-        here = slot(o)
-        return (
-            ref[slot(o - 1), rows, :]
-            + ref[slot(o + 1), rows, :]
-            + ref[here, pl.ds(at - 1, half), :]
-            + ref[here, pl.ds(at + 1, half), :]
-        )
-
-    def relax(ref, o):
-        here = slot(o)
-        top = ref[here, pl.ds(wide_at, half), :]
-        bottom = ref[here, pl.ds(wide_at + half, half), :]
-        tail = ref[here, pl.ds(tail_at, half), :]
-        top_west = pltpu.roll(top, 1, 1)
-        bottom_west = pltpu.roll(bottom, 1, 1)
-        tail_east = pltpu.roll(tail, LANES - 1, 1)
-        total = around(ref, o, wide_at, top)
-        total = total + jnp.where(lane == 0, 0.0, top_west)
-        total = total + jnp.where(lane == LANES - 1, tail_east, pltpu.roll(top, LANES - 1, 1))
-        new_top = 0.1 * top + 0.15 * total
-        total = around(ref, o, wide_at + half, bottom)
-        total = total + jnp.where(lane == 0, 0.0, bottom_west)
-        total = total + jnp.where(
-            lane == LANES - 1, pltpu.roll(tail, rest - 1, 1), pltpu.roll(bottom, LANES - 1, 1)
-        )
-        new_bottom = 0.1 * bottom + 0.15 * total
-        total = around(ref, o, tail_at, tail)
-        west = jnp.where(lane == 0, top_west, pltpu.roll(tail, 1, 1))
-        total = total + jnp.where(lane == rest, pltpu.roll(bottom, rest + 1, 1), west)
-        ends = (lane == rest - 1) | (lane == LANES - 1)
-        total = total + jnp.where(ends, 0.0, tail_east)
-        new_tail = 0.1 * tail + 0.15 * total
-        return new_top, new_bottom, new_tail
-
     @pl.when(step == 0)
     def _():
-        first[...] = jnp.zeros_like(first)
-        second[...] = jnp.zeros_like(second)
+        def wipe(at, _):
+            first[at] = jnp.zeros(first.shape[1:], F32)
+            second[at] = jnp.zeros(second.shape[1:], F32)
+            first_x[at] = jnp.zeros(first_x.shape[1:], F32)
+            second_x[at] = jnp.zeros(second_x.shape[1:], F32)
+            return 0
+
+        lax.fori_loop(0, RING, wipe, 0)
+        row, column = iota(link.shape, 0), iota(link.shape, 1)
+        low, high = jnp.minimum(row, column), jnp.maximum(row, column)
+        split_at = LANES + rest
+        near = (high == low + 1) & (high != split_at)
+        link[...] = jnp.where(near, 1.0, 0.0).astype(BF16)
+        meets = (low == LANES - 1) & (high == split_at)
+        inner = (high == low + 1) & (high < LANES)
+        cross[...] = jnp.where(meets | inner, 1.0, 0.0).astype(BF16)
+
+    def put(ref, at, r, parts):
+        top, bottom, tail = parts
+        ref[at, pl.ds(wide_at + r, piece), :] = top
+        ref[at, pl.ds(wide_at + half + r, piece), :] = bottom
+        ref[at, pl.ds(tail_at + r, piece), :] = tail
+        if r + piece == half:
+            above = pltpu.roll(tail[piece - MARGIN :], LANES - rest, 1)
+            ref[at, pl.ds(tail_at - MARGIN, MARGIN), :] = jnp.where(edge >= rest, above, 0.0)
+        if r == 0:
+            below = pltpu.roll(tail[:MARGIN], LANES - rest, 1)
+            ref[at, pl.ds(tail_at + half, MARGIN), :] = jnp.where(edge < rest, below, 0.0)
+
+    def lateral(ref, sums, at):
+        top = ref[at, pl.ds(wide_at, half), :]
+        bottom = ref[at, pl.ds(wide_at + half, half), :]
+        tail = ref[at, pl.ds(tail_at, half), :]
+        upper = dot(split(jnp.concatenate([top, tail], axis=1)), link[...])
+        joint = dot(split(jnp.concatenate([bottom, tail], axis=1)), cross[...])
+        upper = upper[:half] + upper[half:]
+        joint = joint[:half] + joint[half:]
+        sums[at, pl.ds(0, half), :] = upper[:, :LANES]
+        sums[at, pl.ds(half, half), :] = joint[:, :LANES]
+        sums[at, pl.ds(finest, half), :] = upper[:, LANES:] + joint[:, LANES:]
+
+    def relax(ref, sums, o, r):
+        here, before, after = slot(o), slot(o - 1), slot(o + 1)
+        parts = []
+        for at, side in (
+            (wide_at + r, r), (wide_at + half + r, half + r), (tail_at + r, finest + r)
+        ):
+            rows = pl.ds(at, piece)
+            total = (
+                (ref[before, rows, :] + ref[after, rows, :])
+                + (ref[here, pl.ds(at - 1, piece), :] + ref[here, pl.ds(at + 1, piece), :])
+                + sums[here, pl.ds(side, piece), :]
+            )
+            parts.append(0.1 * ref[here, rows, :] + 0.15 * total)
+        return parts
 
     for o in range(STEP):
-        value = codes[o].astype(F32) * scales[o][:1]
-        if o < 2:
-            value = jnp.where((step == 0) & low, 0.0, value)
-        else:
-            value = jnp.where((step == last) & high, 0.0, value)
-        put(first, slot(o), value[:half], value[half:finest], value[finest:])
+        drop = low_first if o < 2 else high_last
+        scale = jnp.where(drop, 0.0, scales[o][:1])
+        for r in range(0, half, piece):
+            at = (r, half + r, finest + r)
+            put(first, slot(o), r, [codes[o, pl.ds(a, piece), :].astype(F32) * scale for a in at])
+        lateral(first, first_x, slot(o))
 
     for o in range(-1, STEP - 1):
-        parts = relax(first, o)
-        if o == 1:
-            parts = [jnp.where((step == 0) & low, 0.0, p) for p in parts]
-        if o == 2:
-            parts = [jnp.where((step == last) & high, 0.0, p) for p in parts]
-        put(second, slot(o), *parts)
+        for r in range(0, half, piece):
+            parts = relax(first, first_x, o, r)
+            if o == 1:
+                parts = [jnp.where(low_first, 0.0, p) for p in parts]
+            if o == 2:
+                parts = [jnp.where(high_last, 0.0, p) for p in parts]
+            put(second, slot(o), r, parts)
+        lateral(second, second_x, slot(o))
 
     @pl.when(step >= 1)
     def _():
         for o in range(-2, STEP - 2):
-            top, bottom, tail = relax(second, o)
-            out[o + 2, 0:half, 0:LANES] = top
-            out[o + 2, half:finest, 0:LANES] = bottom
-            out[o + 2, 0:half, LANES:finest] = tail[:, :rest]
-            out[o + 2, half:finest, LANES:finest] = pltpu.roll(tail, rest, 1)[:, :rest]
+            for r in range(0, half, piece):
+                top, bottom, tail = relax(second, second_x, o, r)
+                upper, lower = pl.ds(r, piece), pl.ds(half + r, piece)
+                out[o + 2, upper, 0:LANES] = top
+                out[o + 2, lower, 0:LANES] = bottom
+                out[o + 2, upper, LANES:finest] = tail[:, :rest]
+                out[o + 2, lower, LANES:finest] = pltpu.roll(tail, rest, 1)[:, :rest]
 
 
 def sweeps(codes, scales, finest):
@@ -749,13 +848,30 @@
             (STEP, finest, finest), lambda j: (jnp.maximum(j - 1, 0), 0, 0)
         ),
         out_shape=jax.ShapeDtypeStruct((planes, finest, finest), F32),
-        scratch_shapes=[ring, ring],
+        scratch_shapes=[
+            ring,
+            ring,
+            pltpu.VMEM((RING, tall, LANES), F32),
+            pltpu.VMEM((RING, tall, LANES), F32),
+            pltpu.VMEM((2 * LANES, 2 * LANES), BF16),
+            pltpu.VMEM((2 * LANES, 2 * LANES), BF16),
+        ],
         compiler_params=pltpu.CompilerParams(dimension_semantics=("arbitrary",)),
     )(codes, scales)
 
 
 def shards(images, momenta, assign):
-    codes, scales = fused(assign, images, momenta)
+    chips = lax.axis_size("subj") // 2
+    if chips == 2:
+        count = momenta.shape[0]
+        home = jnp.arange(assign.shape[0], dtype=jnp.int32) // (2 * count)
+        crossing = jnp.sum(((home == 0) & (assign // (2 * count) == 1)).astype(jnp.int32))
+        codes, scales = lax.cond(
+            crossing <= 2, functools.partial(fused, 1), functools.partial(fused, 2),
+            assign, images, momenta,
+        )
+    else:
+        codes, scales = fused(2, assign, images, momenta)
     return sweeps(codes, scales, images.shape[2])
 
 

time: 102 us -> 85.7 us (0.84)
  the two profiles are of different devices: /device:TPU:0 before, /device:TPU:17 now
where the time goes in v3:
time: 85.7 us; the launch traced here: 85.2 us
  Pallas kernels  83.2 us (97%)
  other arithmetic  1.3 us (2%)
    pallas_call x1, Pallas kernels, fused(): pl.pallas_call(functools.partial(fused_kernel, messages), out_shape=(jax....  66.7 us
    pallas_call x1, Pallas kernels, sweeps(): pl.pallas_call(sweep_kernel, grid=(planes // STEP + 1,), in_specs=[pl.Blo...  16.5 us

profile of v3, /device:TPU:17, one launch (start us, length us, event | category | flops | bytes accessed | tf_op | source)
XLA Modules:
  0.0 85.2 jit_solution(2959496379655177177)
XLA Ops:
  0.0 1.3 %fusion = s32[]{:T(128)} fusion(s32[8]{0:T(128)} %param.7), kind=kLoop, calls=%fused_computation.9 | loop fusion | flops 223 | bytes 36 | tf_op jit(solution)/shard_map/reduce_sum | solution.py:868
  2.0 66.8 %conditional.1 = ((s16[52,288,128]{2,1,0:T(8,128)(2,1)}, f32[52,8,128]{2,1,0:T(8,128)S(1)})) conditional(s32[]{:T(128)} %convert_element_type.7, (s32[8]{0:T(128)}, bf16[2,48,192,192]{3,2,1,0:T(8,128)(2,1)}, f32[2,24,3,96,96]{4,3,2,1,0:T(8,128)}) %tuple.11, (s32[8]{0:T(128)}, bf16[2,48,192,192]{3,2,1,0:T(8,128)(2,1)}, ...), branch_computations={%region_1.2_spmd, %region_2.3_spmd} | conditional | bytes 8 | solution.py:869
  2.0 66.7 %branch_1_fun.1 = (s16[52,288,128]{2,1,0:T(8,128)(2,1)}, f32[52,8,128]{2,1,0:T(8,128)S(1)}) custom-call(s32[8]{0:T(128)} %get-tuple-element.20.assign, bf16[2,48,192,192]{3,2,1,0:T(8,128)(2,1)} %get-tuple-element.21.images, f32[2,24,3,96,96]{4,3,2,1,0:T(8,128)} %get-tuple-element.22.momenta), custom_call_target="tpu_custom_call" | custom-call | tf_op jit(solution)/shard_map/cond/branch_1_fun/pallas_call | solution.py:711
  68.7 16.5 %shard_map.37 = f32[48,192,192]{2,1,0:T(8,128)} custom-call(s16[52,288,128]{2,1,0:T(8,128)(2,1)} %get-tuple-element.25.codes, f32[52,8,128]{2,1,0:T(8,128)S(1)} %get-tuple-element.26.scales), custom_call_target="tpu_custom_call" | custom-call | tf_op jit(solution)/shard_map/pallas_call | solution.py:840

commit v4 on v3

--- a/solution.py
+++ b/solution.py
@@ -81,7 +81,7 @@
     messages, assign, images, momenta,
     codes, scales,
     up_x, up_y, slope_x, slope_y, blur_x, blur_y,
-    ext, edges, hout, hin, img, vel, ymsg, fine, part, peer, ycode, yscale, mcode, mscale, xcode, xscale,
+    ext, edges, hout, hin, img, vel, ymsg, fine, part, peer, ycode, yscale, mcode, mscale, xcode, xscale, zcode, zscale,
     lsem, hsend, hrecv, vsend, vrecv, qsend, qrecv, psend, precv, ysend, yrecv,
     gsend, grecv, xsend, xrecv, osem, zsend, zrecv,
 ):
@@ -441,6 +441,7 @@
             send.start()
 
     def row_at(n):
+        n = jnp.where(n >= rows_half - 2, 2 * rows_half - 3 - n, n)
         return n + (1 - up) * (rows_half - 1 - 2 * n)
 
     def owned(row):
@@ -451,6 +452,7 @@
     away = 2 + (2 * (1 - level) + core) * planes_block
 
     def block_row(n):
+        n = jnp.where(n >= rows_block - 2, 2 * rows_block - 3 - n, n)
         return n + (1 - up) * (rows_block - 1 - 2 * n)
 
     def spread(here):
@@ -478,18 +480,32 @@
 
     outermost = (level == core) & has_from
     edge_at = pl.ds(level * 2 * (rows_block - 1), 2)
-    edge_out = pl.ds((1 - level) * (fine_slab + 2), 2)
 
     def edge_sends():
         sends = []
-        for m, (a, b) in enumerate(block):
-            for n, (src, dst) in enumerate(((mcode, codes), (mscale, scales))):
+        for m, a in enumerate((1 - level, level)):
+            for n, (src, dst) in enumerate(((mcode, zcode), (mscale, zscale))):
                 sends.append(
                     remote(
-                        src.at[edge_at], dst.at[edge_out], zsend.at[n, m],
-                        zrecv.at[n, 1 - level], (a, b, from_zone),
+                        src.at[edge_at], dst, zsend.at[n, m], zrecv.at[n, 0],
+                        (a, group, from_zone),
                     )
                 )
+        return sends
+
+    has_direct = jnp.where(core == 1, zone, zones - 1 - zone) > 0
+    has_relayed = jnp.where(core == 1, zones - 1 - zone, zone) > 0
+    direct_out = pl.ds((1 - core) * (fine_slab + 2), 2)
+    relayed_out = pl.ds(core * (fine_slab + 2), 2)
+
+    def edge_hands():
+        sends = []
+        for n, (src, dst) in enumerate(((zcode, codes), (zscale, scales))):
+            out = dst.at[direct_out]
+            sends += [
+                remote(src, out, zsend.at[n, 2], zrecv.at[n, 1], mate),
+                pltpu.make_async_copy(src, out, osem.at[n, 2, 0]),
+            ]
         return sends
 
     def publish(here):
@@ -593,14 +609,14 @@
         def _():
             publish(block_row(n))
 
+        @pl.when(outermost & (n == rows_block - 2))
+        def _():
+            for send in edge_sends():
+                send.start()
+
         return 0
 
     lax.fori_loop(0, rows_block, finish, 0)
-
-    @pl.when(outermost)
-    def _():
-        for send in edge_sends():
-            send.start()
 
     def hand(n, _):
         here = rows_block - 1 - block_row(n)
@@ -611,7 +627,16 @@
             send.start()
         return 0
 
-    lax.fori_loop(0, rows_block, hand, 0)
+    lax.fori_loop(0, rows_block - 2, hand, 0)
+
+    @pl.when(has_direct)
+    def _():
+        for n, src in enumerate((zcode, zscale)):
+            remote(src, src, zsend.at[n, 0], zrecv.at[n, 0], me).wait_recv()
+        for send in edge_hands():
+            send.start()
+
+    lax.fori_loop(rows_block - 2, rows_block, hand, 0)
 
     @pl.when(has_to)
     def _():
@@ -646,12 +671,19 @@
         for send in edge_sends():
             send.wait_send()
 
-    for side, there in ((0, has_before), (1, has_after)):
-        @pl.when(there)
-        def _(side=side):
-            out = pl.ds(side * (fine_slab + 2), 2)
-            for n, dst in enumerate((codes, scales)):
-                remote(dst.at[out], dst.at[out], zsend.at[n, 0], zrecv.at[n, side], me).wait_recv()
+    @pl.when(has_direct)
+    def _():
+        for n, send in enumerate(edge_hands()):
+            if n % 2 == 0:
+                send.wait_send()
+            else:
+                send.wait()
+
+    @pl.when(has_relayed)
+    def _():
+        for n, dst in enumerate((codes, scales)):
+            out = dst.at[relayed_out]
+            remote(out, out, zsend.at[n, 0], zrecv.at[n, 1], me).wait_recv()
 
 
 def fused(messages, assign, images, momenta):
@@ -689,6 +721,8 @@
         pltpu.VMEM((planes_block, 8, LANES), F32),
         pltpu.VMEM((planes_block, tall, LANES), jnp.int16),
         pltpu.VMEM((planes_block, 8, LANES), F32),
+        pltpu.VMEM((2, tall, LANES), jnp.int16),
+        pltpu.VMEM((2, 8, LANES), F32),
         dma((3,)),
         dma((2,)),
         dma((2,)),
@@ -704,8 +738,8 @@
         dma((2, 2, rows_block)),
         dma((2, rows_block)),
         dma((2, rows_block)),
-        dma((2, 2, rows_block)),
-        dma((2, 4)),
+        dma((2, 3, rows_block)),
+        dma((2, 3)),
         dma((2, 2)),
     ]
     return pl.pallas_call(

time: 85.7 us -> 84.2 us (0.982)
  the two profiles are of different devices: /device:TPU:17 before, /device:TPU:0 now
where the time goes in v4:
time: 84.2 us; the launch traced here: 83.3 us
  Pallas kernels  81.3 us (97%)
  other arithmetic  1.3 us (2%)
    pallas_call x1, Pallas kernels, fused(): pl.pallas_call(functools.partial(fused_kernel, messages), out_shape=(jax....  64.8 us
    pallas_call x1, Pallas kernels, sweeps(): pl.pallas_call(sweep_kernel, grid=(planes // STEP + 1,), in_specs=[pl.Blo...  16.5 us

profile of v4, /device:TPU:0, one launch (start us, length us, event | category | flops | bytes accessed | tf_op | source)
XLA Modules:
  0.0 83.3 jit_solution(2250645637613250602)
XLA Ops:
  0.0 1.3 %fusion = s32[]{:T(128)} fusion(s32[8]{0:T(128)} %param.7), kind=kLoop, calls=%fused_computation.9 | loop fusion | flops 223 | bytes 36 | tf_op jit(solution)/shard_map/reduce_sum | solution.py:902
  2.0 64.8 %conditional.1 = ((s16[52,288,128]{2,1,0:T(8,128)(2,1)}, f32[52,8,128]{2,1,0:T(8,128)S(1)})) conditional(s32[]{:T(128)} %convert_element_type.7, (s32[8]{0:T(128)}, bf16[2,48,192,192]{3,2,1,0:T(8,128)(2,1)}, f32[2,24,3,96,96]{4,3,2,1,0:T(8,128)}) %tuple.11, (s32[8]{0:T(128)}, bf16[2,48,192,192]{3,2,1,0:T(8,128)(2,1)}, ...), branch_computations={%region_1.2_spmd, %region_2.3_spmd} | conditional | bytes 8 | solution.py:903
  2.0 64.8 %branch_1_fun.1 = (s16[52,288,128]{2,1,0:T(8,128)(2,1)}, f32[52,8,128]{2,1,0:T(8,128)S(1)}) custom-call(s32[8]{0:T(128)} %get-tuple-element.20.assign, bf16[2,48,192,192]{3,2,1,0:T(8,128)(2,1)} %get-tuple-element.21.images, f32[2,24,3,96,96]{4,3,2,1,0:T(8,128)} %get-tuple-element.22.momenta), custom_call_target="tpu_custom_call" | custom-call | tf_op jit(solution)/shard_map/cond/branch_1_fun/pallas_call | solution.py:745
  66.8 16.5 %shard_map.37 = f32[48,192,192]{2,1,0:T(8,128)} custom-call(s16[52,288,128]{2,1,0:T(8,128)(2,1)} %get-tuple-element.25.codes, f32[52,8,128]{2,1,0:T(8,128)S(1)} %get-tuple-element.26.scales), custom_call_target="tpu_custom_call" | custom-call | tf_op jit(solution)/shard_map/pallas_call | solution.py:874
